TPU v7x, 32 devices: a whole 2x2x4 slice. The times are simulated.
32 devices in a mesh: aa: 8 (over y, x, core), ba: 4 (over z).
Axes of the slice: x: 2, y: 2, z: 4, core: 2. Of those that a mesh axis runs over, the one named last changes fastest.
Arguments:
- cotangent: bfloat16 [1, 20, 64, 64, 2048], P(None, None, 'aa', 'ba'), may hold values from -6 to 6
- pre_activations: bfloat16 [2, 1, 20, 64, 64, 2048], P(None, None, None, 'aa', 'ba'), may hold values from -6 to 6
- spectral_weights: bfloat16 [2, 2, 20, 20, 24, 6912], P(None, None, None, None, 'ba', 'aa'), may hold values from -6 to 6
- skip_weights: bfloat16 [2, 20, 20], replicated, may hold values from -1.25 to 1.25
- lift_weights: float32 [20], replicated, may hold values from -1.25 to 1.25
Outputs:
- perm_grad: float32 [1, 64, 64, 2048], P(None, 'aa', 'ba')
All inputs are finite; a program needn't handle non-finite values.
Results may differ from a plain program's by a relative error of at most 0.023.
Values may be sent and summed in bfloat16 or wider, within the bound.
A program may use at most 256 MiB of HBM per device.

v0:
```python
import math

import jax
import jax.numpy as jnp
import numpy as np
from jax import lax
from jax.sharding import PartitionSpec as P

NX = 64
NY = 64
NZ = 64
NT = 32
KX = 24
KY = 24
KZ = 24
KT = 12


def gelu_slope(values):
    normal_cdf = 0.5 * (1.0 + lax.erf(values / math.sqrt(2.0)))
    density = jnp.exp(-0.5 * values * values) / math.sqrt(2.0 * math.pi)
    return normal_cdf + values * density


def signed_freq(total_count):
    index_list = np.arange(total_count)
    return np.where(index_list < total_count // 2, index_list, index_list - total_count)


def line_tables(total_count, length):
    turns = signed_freq(total_count)[:, None] * np.arange(length)[None, :] % length
    angles = 2.0 * math.pi / length * turns
    cosine = np.cos(angles)
    sine_part = np.sin(angles)
    forward = np.stack(
        [np.stack([cosine.T, -sine_part.T], 1), np.stack([sine_part.T, cosine.T], 1)], 0
    )
    inverse = (
        np.stack([np.stack([cosine, sine_part], 1), np.stack([-sine_part, cosine], 1)], 0)
        / length
    )
    return (forward, inverse)


def plane_tables():
    joint_index = np.arange(KZ * KT)
    depth_freq = signed_freq(KZ)[joint_index // KT]
    time_freq = joint_index % KT
    cell_index = np.arange(NZ * NT)
    turns = (
        depth_freq[:, None] * (cell_index // NT)[None, :] * NT
        + time_freq[:, None] * (cell_index % NT)[None, :] * NZ
    ) % (NZ * NT)
    angles = 2.0 * math.pi / (NZ * NT) * turns
    forward = np.stack([np.cos(angles).T, -np.sin(angles).T], 1)
    inverse = np.stack([np.cos(angles), -np.sin(angles)], 0) / (NZ * NT)
    return (forward, inverse)


def rounded_product(pattern, values, table):
    return jnp.einsum(
        pattern, values, jnp.asarray(table, jnp.bfloat16), preferred_element_type=jnp.float32
    )


def exact_product(pattern, values, table):
    return jnp.einsum(
        pattern, values, jnp.asarray(table, jnp.float32), precision=lax.Precision.HIGHEST
    )


def to_bf16(values):
    return values.astype(jnp.bfloat16)


def keep_float(values):
    return values


def exchange(values, axis):
    return lax.all_to_all(values, axis, split_axis=0, concat_axis=0, tiled=True)


def forward_modes(grad_pre, weights, tables):
    plane, first, second = tables
    rows = lax.axis_size("aa")
    columns = lax.axis_size("ba")
    plane = plane.reshape(NZ * NT, 2, rows, -1)
    spectrum = to_bf16(rounded_product("bcxyz,zpnm->nbcpxmy", grad_pre, plane))
    blocks = exchange(spectrum, "aa")
    first = first.reshape(2, rows, NX // rows, 2, columns, KX // columns)
    spectrum = to_bf16(rounded_product("nbcpxmy,pnxqgk->gbcqkmy", blocks, first))
    blocks = exchange(spectrum, "ba")
    second = second.reshape(2, columns, NY // columns, 2, KY)
    result = to_bf16(rounded_product("gbcpkmy,pgyqj->bcqkmj", blocks, second))
    shape = result.shape
    spectrum = result.reshape(shape[:4] + (shape[4] * KY,))
    real_part = spectrum[:, :, 0]
    imag_part = spectrum[:, :, 1]

    def mixing(values, matrix):
        return jnp.einsum("bokr,oikr->bikr", values, matrix, preferred_element_type=jnp.float32)

    result_real = mixing(real_part, weights[0]) + mixing(imag_part, weights[1])
    result_imag = mixing(imag_part, weights[0]) - mixing(real_part, weights[1])
    return jnp.stack([result_real, result_imag], 2)


def back_path(mode_values, tables, multiply, finish):
    first, second, plane = tables
    rows = lax.axis_size("aa")
    columns = lax.axis_size("ba")
    extent = mode_values.shape
    gridded = mode_values.reshape(extent[:4] + (extent[4] // KY, KY))
    second = second.reshape(2, KY, 2, columns, NY // columns)
    blocks = exchange(finish(multiply("bcpkmj,pjqgu->gbcqkmu", gridded, second)), "ba")
    first = first.reshape(2, columns, KX // columns, 2, rows, NX // rows)
    back = to_bf16(multiply("gbcpkmu,pgkqnx->nbcqxmu", blocks, first))
    blocks = exchange(back, "aa")
    plane = plane.reshape(2, rows, -1, NZ * NT)
    return rounded_product("nbcpxmu,pnmz->bcxuz", blocks, plane)


def per_device(cotangent, pre_activations, spectral_weights, skip_weights, lift_weights):
    plane_forward, plane_inverse = plane_tables()
    first_forward, first_inverse = line_tables(KX, NX)
    second_forward, second_inverse = line_tables(KY, NY)
    forward_tables = (plane_forward, first_forward, second_forward)
    back_tables = (first_inverse, second_inverse, plane_inverse)
    incoming = cotangent.astype(jnp.float32)
    layers = pre_activations.shape[0]
    perm_grad = None
    for layer_index in range(layers - 1, -1, -1):
        slope = gelu_slope(pre_activations[layer_index].astype(jnp.float32))
        grad_pre = (incoming * slope).astype(jnp.bfloat16)
        mode_values = forward_modes(grad_pre, spectral_weights[layer_index], forward_tables)
        if layer_index > 0:
            skip_term = jnp.einsum(
                "boxyz,oi->bixyz",
                grad_pre,
                skip_weights[layer_index],
                preferred_element_type=jnp.float32,
            )
            spectral = back_path(
                mode_values.astype(jnp.bfloat16), back_tables, rounded_product, to_bf16
            )
            incoming = skip_term + spectral
        else:
            folded = jnp.sum(mode_values * lift_weights[None, :, None, None, None], 1)[:, None]
            spectral = back_path(folded, back_tables, exact_product, keep_float)
            combined = jnp.sum(skip_weights[0].astype(jnp.float32) * lift_weights[None, :], 1)
            projected = jnp.sum(
                grad_pre.astype(jnp.float32) * combined[None, :, None, None, None], 1
            )
            perm_grad = projected + spectral[:, 0]
    return perm_grad


def solution(mesh):
    return jax.shard_map(
        per_device,
        mesh=mesh,
        in_specs=(
            P(None, None, "aa", "ba", None),
            P(None, None, None, "aa", "ba", None),
            P(None, None, None, None, "ba", "aa"),
            P(),
            P(),
        ),
        out_specs=P(None, "aa", "ba", None),
        check_vma=False,
    )
```

profile of v0, /device:TPU:0, one launch (start us, length us, event | category | flops | bytes accessed | tf_op | source)
XLA Modules:
  0.0 751.2 jit_solution(14171039238767741179)
XLA Ops:
  0.0 11.8 %fusion.15 = bf16[1,20,8,16,2048]{4,3,2,1,0:T(8,128)(2,1)S(1)} fusion(bf16[1,20,8,16,2048]{4,3,2,1,0:T(8,128)(2,1)} %param.17, bf16[2,1,20,8,16,2048]{5,4,3,2,1,0:T(8,128)(2,1)} %param.18), kind=kLoop, calls=%fused_computation.26 | loop fusion | flops 62914560 | bytes 31457280 | tf_op jit(solution)/shard_map/convert_element_type | solution.py:135
  15.7 24.3 %convert_bitcast_fusion.1 = bf16[8,1,20,2,8,36,16]{5,6,0,3,4,2,1:T(8,128)(2,1)} fusion(bf16[2048,2,8,36,1,1]{0,3,2,1,5,4:T(8,128)(2,1)S(1)} %copy-done.9, bf16[1,20,8,16,2048]{4,3,2,1,0:T(8,128)(2,1)S(1)} %fusion.15), kind=kOutput, calls=%fused_computation.54 | convolution fusion | flops 6041272320 | bytes 15794176 | tf_op jit(solution)/shard_map/bcxyz,zpnm->nbcpxmy/dot_general | solution.py:61
  39.9 10.9 %copy.358 = bf16[8,1,20,2,8,36,16]{5,6,3,4,2,1,0:T(8,128)(2,1)} copy(bf16[8,1,20,2,8,36,16]{5,6,0,3,4,2,1:T(8,128)(2,1)} %convert_bitcast_fusion.1) | data formatting | bytes 5898240 | tf_op jit(solution)/shard_map/convert_element_type | solution.py:73
  50.9 25.2 %reshape.320 = bf16[8,2,92160]{2,1,0:T(2,128)(2,1)S(1)} reshape(bf16[8,1,20,8,2,16,36]{6,5,4,3,2,1,0:T(8,128)(2,1)} %bitcast.398) | data formatting | bytes 5898240
  76.1 41.4 %all_to_all.40 = bf16[8,2,92160]{2,1,0:T(2,128)(2,1)} all-to-all(bf16[8,2,92160]{2,1,0:T(2,128)(2,1)S(1)} %reshape.320), channel_id=1, replica_groups=mesh['aa'=8,'ba'=4] {'aa'}, dimensions={0} | all-to-all | bytes 5898240 | tf_op jit(solution)/shard_map/all_to_all | solution.py:81
  117.5 30.4 %reshape.321 = bf16[8,1,20,8,2,16,36]{6,5,4,3,2,1,0:T(8,128)(2,1)} reshape(bf16[8,2,92160]{2,1,0:T(2,128)(2,1)} %all_to_all.40) | data formatting | bytes 5898240
  178.4 34.9 %fusion.85 = (bf16[1,1,20,20,6,864]{5,1,4,3,2,0:T(2,128)(2,1)}, bf16[1,1,20,20,6,864]{5,1,4,3,2,0:T(2,128)(2,1)}, bf16[1,1,20,20,6,864]{5,1,4,3,2,0:T(2,128)(2,1)}, bf16[1,1,20,20,6,864]{5,1,4,3,2,0:T(2,128)(2,1)}) fusion(bf16[2,2,20,20,6,864]{5,1,4,3,2,0:T(2,128)(2,1)} %param.19), kind=kLoop, calls=%fused_computation.114 | loop fusion | bytes 33177600 | tf_op jit(solution)/shard_map/slice | solution.py:104
  213.3 11.9 %reshape.323 = bf16[4,1,20,2,6,16,36]{6,5,4,3,2,1,0:T(8,128)(2,1)} reshape(bf16[4,2,69120]{2,1,0:T(2,128)(2,1)S(1)} %all-to-all-done.1) | data formatting | bytes 2211840
  236.3 13.7 %fusion.33 = (f32[6,864,20]{1,2,0:T(8,128)S(1)}, f32[6,864,20]{1,2,0:T(8,128)S(1)}, f32[6,864,20]{1,2,0:T(8,128)S(1)}, f32[6,864,20]{1,2,0:T(8,128)S(1)}) fusion(f32[6,864,20]{1,0,2:T(8,128)S(1)} %copy.260, bf16[1,1,20,20,6,864]{5,1,4,3,2,0:T(2,128)(2,1)} %get-tuple-element.20, f32[6,864,20]{1,0,2:T(8,128)S(1)} %copy.261, ...), kind=kLoop, calls=%fused_computation.55 | loop fusion | flops 20321280 | bytes 10782720 | tf_op jit(solution)/shard_map/bokr,oikr->bikr/dot_general | solution.py:102
  267.8 31.6 %all_to_all.41 = bf16[4,2,69120]{2,1,0:T(2,128)(2,1)S(1)} all-to-all(bf16[4,2,69120]{2,1,0:T(2,128)(2,1)S(1)} %reshape.324), channel_id=1, replica_groups=mesh['aa'=8,'ba'=4] {'ba'}, dimensions={0} | all-to-all | bytes 2211840 | tf_op jit(solution)/shard_map/all_to_all | solution.py:81
  299.5 11.9 %reshape.325 = bf16[4,1,20,6,2,16,36]{6,5,4,3,2,1,0:T(8,128)(2,1)} reshape(bf16[4,2,69120]{2,1,0:T(2,128)(2,1)S(1)} %all_to_all.41) | data formatting | bytes 2211840
  330.5 26.0 %reshape.326 = bf16[8,2,92160]{2,1,0:T(2,128)(2,1)} reshape(bf16[8,1,20,16,2,8,36]{6,5,4,3,2,1,0:T(8,128)(2,1)} %bitcast.399) | data formatting | bytes 5898240
  370.8 19.2 %fusion.20 = f32[8,16,2048,20]{2,3,1,0:T(8,128)} fusion(bf16[20,8,16,2048]{3,2,1,0:T(8,128)(2,1)} %bitcast.397, bf16[1,20,20]{1,2,0:T(8,128)(2,1)S(1)} %copy.253), kind=kOutput, calls=%fused_computation.38 | convolution fusion | flops 209715200 | bytes 31458080 | tf_op jit(solution)/shard_map/boxyz,oi->bixyz/dot_general | solution.py:138
  396.0 30.9 %reshape.327 = bf16[8,1,20,16,2,8,36]{6,5,4,3,2,1,0:T(8,128)(2,1)} reshape(bf16[8,2,92160]{2,1,0:T(2,128)(2,1)S(1)} %all-to-all-done.3) | data formatting | bytes 5898240
  426.9 12.0 %bitcast_bitcast_fusion = bf16[8,20,2,8,36,16]{4,3,2,5,1,0:T(8,128)(2,1)} fusion(bf16[8,1,20,16,2,8,36]{6,5,4,3,2,1,0:T(8,128)(2,1)} %reshape.327), kind=kLoop, calls=%fused_computation.118 | loop fusion | bytes 5898240 | tf_op jit(solution)/shard_map/reshape.28
  438.9 52.2 %multiply_reduce_fusion = (f32[8,16,2048]{2,1,0:T(8,128)}, bf16[20,8,16,2048]{3,0,2,1:T(8,128)(2,1)}) fusion(f32[20]{0:T(128)S(1)} %fusion.82, bf16[1,1,20,8,16,2048]{5,4,3,2,1,0:T(8,128)(2,1)} %slice.56, bf16[2,8,36,2048,1,1]{3,2,0,1,5,4:T(8,128)(2,1)} %constant.54, bf16[8,20,2,8,36,16]{4,3,2,5,1,0:T(8,128)(2,1)} %bitcast_bitcast_fusion, ...), kind=kOutput, calls=%fused_computation.16 | convolution fusion | flops 6118178816 | bytes 48300112 | tf_op jit(solution)/shard_map/nbcpxmu,pnmz->bcxuz/dot_general | solution.py:61
  491.1 32.6 %convert_bitcast_fusion = bf16[8,1,20,2,8,36,16]{5,6,0,3,4,2,1:T(8,128)(2,1)} fusion(bf16[2048,2,8,36,1,1]{0,3,2,1,5,4:T(8,128)(2,1)S(1)} %copy-done.10, bf16[20,8,16,2048,1,1]{3,0,2,1,5,4:T(8,128)(2,1)} %bitcast.411), kind=kOutput, calls=%fused_computation.53 | convolution fusion | flops 6041272320 | bytes 15794176 | tf_op jit(solution)/shard_map/bcxyz,zpnm->nbcpxmy/dot_general | solution.py:61
  523.8 10.9 %copy.356 = bf16[8,1,20,2,8,36,16]{5,6,3,4,2,1,0:T(8,128)(2,1)} copy(bf16[8,1,20,2,8,36,16]{5,6,0,3,4,2,1:T(8,128)(2,1)} %convert_bitcast_fusion) | data formatting | bytes 5898240 | tf_op jit(solution)/shard_map/convert_element_type | solution.py:73
  534.7 25.2 %reshape.328 = bf16[8,2,92160]{2,1,0:T(2,128)(2,1)S(1)} reshape(bf16[8,1,20,8,2,16,36]{6,5,4,3,2,1,0:T(8,128)(2,1)} %bitcast.400) | data formatting | bytes 5898240
  559.9 39.2 %all_to_all.42 = bf16[8,2,92160]{2,1,0:T(2,128)(2,1)} all-to-all(bf16[8,2,92160]{2,1,0:T(2,128)(2,1)S(1)} %reshape.328), channel_id=1, replica_groups=mesh['aa'=8,'ba'=4] {'aa'}, dimensions={0} | all-to-all | bytes 5898240 | tf_op jit(solution)/shard_map/all_to_all | solution.py:81
  599.2 30.4 %reshape.329 = bf16[8,1,20,8,2,16,36]{6,5,4,3,2,1,0:T(8,128)(2,1)} reshape(bf16[8,2,92160]{2,1,0:T(2,128)(2,1)} %all_to_all.42) | data formatting | bytes 5898240
  654.3 29.8 %all_to_all.43 = bf16[4,2,69120]{2,1,0:T(2,128)(2,1)S(1)} all-to-all(bf16[4,2,69120]{2,1,0:T(2,128)(2,1)S(1)} %reshape.330), channel_id=1, replica_groups=mesh['aa'=8,'ba'=4] {'ba'}, dimensions={0} | all-to-all | bytes 2211840 | tf_op jit(solution)/shard_map/all_to_all | solution.py:81
  684.1 11.9 %reshape.331 = bf16[4,1,20,2,6,16,36]{6,5,4,3,2,1,0:T(8,128)(2,1)} reshape(bf16[4,2,69120]{2,1,0:T(2,128)(2,1)S(1)} %all_to_all.43) | data formatting | bytes 2211840
  707.1 13.7 %fusion.37 = (f32[6,864,20]{1,2,0:T(8,128)S(1)}, f32[6,864,20]{1,2,0:T(8,128)S(1)}, f32[6,864,20]{1,2,0:T(8,128)S(1)}, f32[6,864,20]{1,2,0:T(8,128)S(1)}) fusion(f32[6,864,20]{1,0,2:T(8,128)S(1)} %copy.262, bf16[1,1,20,20,6,864]{5,1,4,3,2,0:T(2,128)(2,1)} %get-tuple-element.18, f32[6,864,20]{1,0,2:T(8,128)S(1)} %copy.263, ...), kind=kLoop, calls=%fused_computation.59 | loop fusion | flops 20321280 | bytes 10782720 | tf_op jit(solution)/shard_map/bokr,oikr->bikr/dot_general | solution.py:102
  (87 shorter events, 167.9 us)
Async XLA Ops:
  0.0 15.7 %copy-start.9 = (bf16[2048,2,8,36,1,1]{0,3,2,1,5,4:T(8,128)(2,1)S(1)}, bf16[2048,2,8,36,1,1]{0,3,2,1,5,4:T(8,128)(2,1)}, u32[]{:S(2)}) copy-start(bf16[2048,2,8,36,1,1]{0,3,2,1,5,4:T(8,128)(2,1)} %constant.49) | copy-start | bytes 7077892
  11.8 3.9 copy-start
  76.1 71.8 %copy-start.11 = (bf16[2,8,8,2,4,6,1,1]{2,5,0,1,4,3,7,6:T(8,128)(2,1)S(1)}, bf16[2,8,8,2,4,6,1,1]{2,5,0,1,4,3,7,6:T(8,128)(2,1)}, u32[]{:S(2)}) copy-start(bf16[2,8,8,2,4,6,1,1]{2,5,0,1,4,3,7,6:T(8,128)(2,1)} %constant.50) | copy-start | bytes 36868
  173.3 40.0 %all-to-all-start.1 = ((bf16[4,2,69120]{2,1,0:T(2,128)(2,1)}), bf16[4,2,69120]{2,1,0:T(2,128)(2,1)S(1)}, u32[]{:S(2)}, u32[]{:S(2)}) async-start(bf16[4,2,69120]{2,1,0:T(2,128)(2,1)} %reshape.322), calls=%async_computation.1 | async-start | bytes 2211840 | tf_op jit(solution)/shard_map/all_to_all | solution.py:81
  178.4 46.9 %copy-start.1 = (bf16[2,4,16,2,24,1,1]{4,2,0,1,3,6,5:T(8,128)(2,1)S(1)}, bf16[2,4,16,2,24,1,1]{4,2,0,1,3,6,5:T(8,128)(2,1)}, u32[]{:S(2)}) copy-start(bf16[2,4,16,2,24,1,1]{4,2,0,1,3,6,5:T(8,128)(2,1)} %constant.51) | copy-start | bytes 36868
  236.3 17.7 %copy-start.4 = (bf16[2,24,2,4,16,1,1]{1,4,0,3,2,6,5:T(8,128)(2,1)S(1)}, bf16[2,24,2,4,16,1,1]{1,4,0,3,2,6,5:T(8,128)(2,1)}, u32[]{:S(2)}) copy-start(bf16[2,24,2,4,16,1,1]{1,4,0,3,2,6,5:T(8,128)(2,1)} %constant.52) | copy-start | bytes 36868
  255.3 56.1 %copy-start.13 = (bf16[2,4,6,2,8,8,1,1]{2,5,0,1,4,3,7,6:T(8,128)(2,1)S(1)}, bf16[2,4,6,2,8,8,1,1]{2,5,0,1,4,3,7,6:T(8,128)(2,1)}, u32[]{:S(2)}) copy-start(bf16[2,4,6,2,8,8,1,1]{2,5,0,1,4,3,7,6:T(8,128)(2,1)} %constant.53) | copy-start | bytes 36868
  356.5 39.5 %all-to-all-start.3 = ((bf16[8,2,92160]{2,1,0:T(2,128)(2,1)}), bf16[8,2,92160]{2,1,0:T(2,128)(2,1)S(1)}, u32[]{:S(2)}, u32[]{:S(2)}) async-start(bf16[8,2,92160]{2,1,0:T(2,128)(2,1)} %reshape.326), calls=%async_computation.3 | async-start | bytes 5898240 | tf_op jit(solution)/shard_map/all_to_all | solution.py:81
  360.3 10.2 %copy-start.5 = (bf16[2,20,20]{2,0,1:T(2,128)(2,1)S(1)}, bf16[2,20,20]{2,0,1:T(2,128)(2,1)}, u32[]{:S(2)}) copy-start(bf16[2,20,20]{2,0,1:T(2,128)(2,1)} %param.20) | copy-start | bytes 4804
  360.3 10.3 %copy-start.6 = (f32[20]{0:T(128)S(1)}, f32[20]{0:T(128)}, u32[]{:S(2)}) copy-start(f32[20]{0:T(128)} %param.21) | copy-start | bytes 244
  438.9 52.2 %copy-start.10 = (bf16[2048,2,8,36,1,1]{0,3,2,1,5,4:T(8,128)(2,1)S(1)}, bf16[2048,2,8,36,1,1]{0,3,2,1,5,4:T(8,128)(2,1)}, u32[]{:S(2)}) copy-start(bf16[2048,2,8,36,1,1]{0,3,2,1,5,4:T(8,128)(2,1)} %constant.49) | copy-start | bytes 7077892
  559.9 69.7 %copy-start.12 = (bf16[2,8,8,2,4,6,1,1]{2,5,0,1,4,3,7,6:T(8,128)(2,1)S(1)}, bf16[2,8,8,2,4,6,1,1]{2,5,0,1,4,3,7,6:T(8,128)(2,1)}, u32[]{:S(2)}) copy-start(bf16[2,8,8,2,4,6,1,1]{2,5,0,1,4,3,7,6:T(8,128)(2,1)} %constant.50) | copy-start | bytes 36868
  638.4 57.7 %copy-start.2 = (bf16[2,4,16,2,24,1,1]{4,2,0,1,3,6,5:T(8,128)(2,1)S(1)}, bf16[2,4,16,2,24,1,1]{4,2,0,1,3,6,5:T(8,128)(2,1)}, u32[]{:S(2)}) copy-start(bf16[2,4,16,2,24,1,1]{4,2,0,1,3,6,5:T(8,128)(2,1)} %constant.51) | copy-start | bytes 36868
  707.1 14.8 %copy-start.7 = (f32[20]{0:T(128)S(1)}, f32[20]{0:T(128)}, u32[]{:S(2)}) copy-start(f32[20]{0:T(128)} %param.21) | copy-start | bytes 244
  707.1 15.9 %copy-start.3 = (f32[2,24,2,4,16,1]{1,4,0,5,3,2:T(8,128)S(1)}, f32[2,24,2,4,16,1]{1,4,0,5,3,2:T(8,128)}, u32[]{:S(2)}) copy-start(f32[2,24,2,4,16,1]{1,4,0,5,3,2:T(8,128)} %constant.55) | copy-start | bytes 73732
  720.9 26.8 %copy-start.8 = (bf16[2,8,36,2048,1]{3,2,0,4,1:T(8,128)(2,1)S(1)}, bf16[2,8,36,2048,1]{3,2,0,4,1:T(8,128)(2,1)}, u32[]{:S(2)}) copy-start(bf16[2,8,36,2048,1]{3,2,0,4,1:T(8,128)(2,1)} %constant.57) | copy-start | bytes 7077892
where the time goes:
time: 760 us; the launch traced here: 751 us
  local copies, waits for them, and re-layouts  366 us (48%)
  matrix products  169 us (22%)
  blocking collectives  158 us (21%)
  other arithmetic  41.7 us (5%)
  starting transfers between devices  8.86 us (1%)
    unnamed x49, local copies, waits for them, and re-layouts  241 us
    all_to_all x6, blocking collectives, exchange(): return lax.all_to_all(values, axis, split_axis=0, concat_axis=0, tiled=True)  158 us
    dot_general x10, matrix products, rounded_product(): jnp.einsum(pattern, values, jnp.asarray(table, jnp.bfloat16), preferred_e...  147 us
    convert_element_type x9, local copies, waits for them, and re-layouts, to_bf16(): return values.astype(jnp.bfloat16)  55.2 us
    slice x1, local copies, waits for them, and re-layouts, forward_modes(): result_real = mixing(real_part, weights[0]) + mixing(imag_part, weights[1])  34.9 us
    dot_general x2, other arithmetic, mixing(): jnp.einsum('bokr,oikr->bikr', values, matrix, preferred_element_type=jnp....  27.4 us
    dot_general x1, matrix products, per_device(): jnp.einsum('boxyz,oi->bixyz', grad_pre, skip_weights[layer_index], prefer...  19.2 us
  transfers between devices with their start and end apart: 2, of which 1 were waited for; matrix products, arithmetic and copies ran while one was open for 9% of the time, Pallas kernels for 0%

commit v1 on v0

--- a/solution.py
+++ b/solution.py
@@ -1,9 +1,12 @@
+import functools
 import math
 
 import jax
 import jax.numpy as jnp
 import numpy as np
 from jax import lax
+from jax.experimental import pallas as pl
+from jax.experimental.pallas import tpu as pltpu
 from jax.sharding import PartitionSpec as P
 
 NX = 64
@@ -121,7 +124,7 @@
     return rounded_product("nbcpxmu,pnmz->bcxuz", blocks, plane)
 
 
-def per_device(cotangent, pre_activations, spectral_weights, skip_weights, lift_weights):
+def per_device_plain(cotangent, pre_activations, spectral_weights, skip_weights, lift_weights):
     plane_forward, plane_inverse = plane_tables()
     first_forward, first_inverse = line_tables(KX, NX)
     second_forward, second_inverse = line_tables(KY, NY)
@@ -156,9 +159,511 @@
     return perm_grad
 
 
+F32 = jnp.float32
+BF16 = jnp.bfloat16
+MESH = pl.DeviceIdType.MESH
+
+
+class Plan:
+    def __init__(self, mesh, channels):
+        self.rows = mesh.shape["aa"]
+        self.columns = mesh.shape["ba"]
+        self.xb = NX // self.rows
+        self.yb = NY // self.columns
+        self.mb = KZ * KT // self.rows
+        self.kb = KX // self.columns
+        self.cells = NZ * NT
+        self.spots = self.xb * self.yb
+        self.channels = channels
+        self.group = 4
+        self.groups = channels // self.group
+        self.tall = self.group * self.mb
+        self.half = 128
+        self.kpad = self.half // self.yb
+        self.modes = 2 * self.kb * KY
+
+    def fits(self):
+        return (
+            self.spots == self.half
+            and self.half % self.yb == 0
+            and self.yb % 16 == 0
+            and self.kb <= self.kpad
+            and self.channels % self.group == 0
+            and self.tall % 16 == 0
+            and self.xb % 2 == 0
+        )
+
+
+def real_form(matrix):
+    top = np.stack([matrix.real, matrix.imag], 1)
+    low = np.stack([-matrix.imag, matrix.real], 1)
+    return np.stack([top, low], 0)
+
+
+def line_phase(count, length):
+    turns = signed_freq(count)[:, None] * np.arange(length)[None, :] % length
+    return np.exp(2j * math.pi * turns / length)
+
+
+def dense_tables(plan):
+    rows, columns = plan.rows, plan.columns
+    eye_y = np.eye(plan.yb)
+    eye_k = np.eye(plan.kpad)[: plan.kb]
+    along_x = line_phase(KX, NX)
+    along_y = line_phase(KY, NY)
+    plane_forward, plane_inverse = plane_tables()
+    tables = {}
+    tables["plane_in"] = plane_forward.transpose(1, 2, 0).reshape(2 * KZ * KT, plan.cells)
+    part = real_form(along_x.conj().T).reshape(2, rows, plan.xb, 2, columns, plan.kb)
+    wide = np.einsum("psxqgk,yw,kl->spxygqlw", part, eye_y, eye_k)
+    tables["x_in"] = wide.reshape(rows * 2 * plan.spots, columns * 2 * plan.half)
+    part = real_form(along_y.conj().T).reshape(2, columns, plan.yb, 2, KY)
+    wide = np.einsum("pbyqj,kl->bplyqkj", part, eye_k)
+    tables["y_in"] = wide.reshape(columns * 2 * plan.half, plan.modes)
+    part = (real_form(along_y) / NY).reshape(2, KY, 2, columns, plan.yb)
+    wide = np.einsum("pjqhy,kl->pkjhqly", part, eye_k)
+    tables["y_out"] = wide.reshape(plan.modes, columns * 2 * plan.half)
+    part = (real_form(along_x) / NX).reshape(2, columns, plan.kb, 2, rows, plan.xb)
+    wide = np.einsum("pbkqnx,yw,kl->bplynqxw", part, eye_y, eye_k)
+    tables["x_out"] = wide.reshape(columns * 2 * plan.half, rows * 2 * plan.spots)
+    back = plane_inverse.reshape(2, rows, plan.mb, plan.cells).transpose(1, 0, 2, 3)
+    tables["plane_out"] = back.reshape(2 * KZ * KT, plan.cells)
+    return {name: jnp.asarray(table.astype(jnp.bfloat16)) for name, table in tables.items()}
+
+
+def product(left, right, contract=((1,), (0,))):
+    return lax.dot_general(left, right, (contract, ((), ())), preferred_element_type=F32)
+
+
+def greet(plan):
+    barrier = pltpu.get_barrier_semaphore()
+    for axis, size in (("aa", plan.rows), ("ba", plan.columns)):
+        for hop in range(1, size):
+            peer = lax.rem(lax.axis_index(axis) + hop, size)
+            pl.semaphore_signal(barrier, inc=1, device_id={axis: peer}, device_id_type=MESH)
+    pl.semaphore_wait(barrier, plan.rows + plan.columns - 2)
+
+
+class Exchange:
+    def __init__(self, axis, size, out, into, sent, came):
+        self.axis, self.size = axis, size
+        self.out, self.into, self.sent, self.came = out, into, sent, came
+
+    def copy(self, group, hop):
+        me = lax.axis_index(self.axis)
+        peer = lax.rem(me + hop, self.size)
+        return pltpu.make_async_remote_copy(
+            src_ref=self.out.at[group, peer],
+            dst_ref=self.into.at[group, me],
+            send_sem=self.sent.at[group, hop],
+            recv_sem=self.came.at[group, hop],
+            device_id={self.axis: peer},
+            device_id_type=MESH,
+        )
+
+    def start(self, group):
+        for hop in range(1, self.size):
+            self.copy(group, hop).start()
+        me = lax.axis_index(self.axis)
+        self.into[group, me] = self.out[group, me]
+
+    def arrive(self, group):
+        for hop in range(1, self.size):
+            self.copy(group, hop).wait_recv()
+
+    def finish(self, groups):
+        def drain(group, carry):
+            for hop in range(1, self.size):
+                self.copy(group, hop).wait_send()
+            return carry
+
+        lax.fori_loop(0, groups, drain, 0)
+
+
+def exchange_scratch(plan, groups, tall):
+    rows, columns = plan.rows, plan.columns
+    return [
+        pltpu.VMEM((groups, rows, tall, 2 * plan.spots), BF16),
+        pltpu.VMEM((groups, rows, tall, 2 * plan.spots), BF16),
+        pltpu.SemaphoreType.DMA((groups, rows)),
+        pltpu.SemaphoreType.DMA((groups, rows)),
+        pltpu.VMEM((groups, columns, tall, 2 * plan.half), BF16),
+        pltpu.VMEM((groups, columns, tall, 2 * plan.half), BF16),
+        pltpu.SemaphoreType.DMA((groups, columns)),
+        pltpu.SemaphoreType.DMA((groups, columns)),
+    ]
+
+
+def exchanges(plan, scratch):
+    return (
+        Exchange("aa", plan.rows, *scratch[:4]),
+        Exchange("ba", plan.columns, *scratch[4:8]),
+    )
+
+
+def plane_in(plan, group, values, table, wide, over_a):
+    rows, mb, spots = plan.rows, plan.mb, plan.spots
+    wide[...] = product(table[...], values, ((1,), (1,)))
+    for owner in range(rows):
+        halves = []
+        for part in range(2):
+            first = (part * rows + owner) * mb
+            halves.append(
+                jnp.concatenate(
+                    [
+                        wide[first : first + mb, c * spots : (c + 1) * spots]
+                        for c in range(plan.group)
+                    ],
+                    0,
+                )
+            )
+        over_a.out[group, owner] = jnp.concatenate(halves, 1).astype(BF16)
+    over_a.start(group)
+
+
+def joined(ref, group, size):
+    return jnp.concatenate([ref[group, index] for index in range(size)], 1)
+
+
+def x_in(plan, group, table, over_a, over_b):
+    over_a.arrive(group)
+    result = product(joined(over_a.into, group, plan.rows), table[...]).astype(BF16)
+    width = 2 * plan.half
+    for owner in range(plan.columns):
+        over_b.out[group, owner] = result[:, owner * width : (owner + 1) * width]
+    over_b.start(group)
+
+
+def y_in(plan, group, table, over_b, spectrum):
+    over_b.arrive(group)
+    result = product(joined(over_b.into, group, plan.columns), table[...])
+    spectrum[0] = result.astype(BF16)
+
+
+def y_out(plan, group, values, table, over_b):
+    result = product(values, table[...]).astype(BF16)
+    width = 2 * plan.half
+    for owner in range(plan.columns):
+        over_b.out[group, owner] = result[:, owner * width : (owner + 1) * width]
+    over_b.start(group)
+
+
+def x_out(plan, group, table, over_b, over_a):
+    over_b.arrive(group)
+    values = joined(over_b.into, group, plan.columns)
+    width = 2 * plan.spots
+    for owner in range(plan.rows):
+        cut = table[:, owner * width : (owner + 1) * width]
+        over_a.out[group, owner] = product(values, cut).astype(BF16)
+    over_a.start(group)
+
+
+def plane_out(plan, group, count, table, over_a):
+    over_a.arrive(group)
+    mb, spots = plan.mb, plan.spots
+    pieces = []
+    for source in range(plan.rows):
+        block = over_a.into[group, source].astype(F32)
+        for part in range(2):
+            pieces.append(
+                jnp.concatenate(
+                    [
+                        block[c * mb : (c + 1) * mb, part * spots : (part + 1) * spots]
+                        for c in range(count)
+                    ],
+                    1,
+                )
+            )
+    values = jnp.concatenate(pieces, 0).astype(BF16)
+    return product(values, table[...], ((0,), (0,)))
+
+
+def forward_kernel(plan, cotangent, pre, t_plane, t_x, t_y, mix, skip, spectrum, field, wide, *scratch):
+    step = pl.program_id(0)
+    over_a, over_b = exchanges(plan, scratch)
+    groups, group = plan.groups, plan.group
+    lanes = 512
+
+    @pl.when(step == 0)
+    def _():
+        greet(plan)
+
+    @pl.when(step < groups)
+    def _():
+        def line(index, carry):
+            c = index // plan.xb
+            x = index % plan.xb
+            for first in range(0, plan.cells, lanes):
+                cut = pl.ds(first, lanes)
+                slope = gelu_slope(pre[0, 0, c, x, :, cut].astype(F32))
+                value = cotangent[0, c, x, :, cut].astype(F32) * slope
+                field[step * group + c, x, :, cut] = value.astype(BF16)
+            return carry
+
+        lax.fori_loop(0, group * plan.xb, line, 0)
+        values = field[pl.ds(step * group, group)].reshape(group * plan.spots, plan.cells)
+        plane_in(plan, step, values, t_plane, wide, over_a)
+
+    @pl.when(step >= groups)
+    def _():
+        def line(index, carry):
+            x = (step - groups) * (plan.xb // 2) + index
+            for first in range(0, plan.cells, lanes):
+                cut = pl.ds(first, lanes)
+                values = field[:, x, :, cut].reshape(plan.channels * plan.yb, lanes)
+                result = product(mix[...], values).astype(BF16)
+                skip[:, index, :, cut] = result.reshape(plan.channels, plan.yb, lanes)
+            return carry
+
+        lax.fori_loop(0, plan.xb // 2, line, 0)
+
+    @pl.when(jnp.logical_and(step >= 1, step <= groups))
+    def _():
+        x_in(plan, step - 1, t_x, over_a, over_b)
+
+    @pl.when(step >= 2)
+    def _():
+        y_in(plan, step - 2, t_y, over_b, spectrum)
+
+    @pl.when(step == groups + 1)
+    def _():
+        over_a.finish(groups)
+        over_b.finish(groups)
+
+
+def middle_kernel(
+    plan, modes, skip, pre, weight, t_plane, t_x, t_y, s_y, s_x, s_plane,
+    spectrum, projected, values, wide, *scratch,
+):
+    step = pl.program_id(0)
+    back_a, back_b = exchanges(plan, scratch[:8])
+    over_a, over_b = exchanges(plan, scratch[8:])
+    groups, group = plan.groups, plan.group
+    lanes = 512
+
+    @pl.when(step == 0)
+    def _():
+        greet(plan)
+
+        def send(index, carry):
+            y_out(plan, index, modes[index], s_y, back_b)
+            return carry
+
+        lax.fori_loop(0, groups, send, 0)
+        projected[...] = jnp.zeros_like(projected)
+
+    @pl.when(step < groups)
+    def _():
+        x_out(plan, step, s_x, back_b, back_a)
+
+    @pl.when(jnp.logical_and(step >= 1, step <= groups))
+    def _():
+        at = step - 1
+        values[...] = plane_out(plan, at, group, s_plane, back_a)
+
+        def line(index, carry):
+            c = index // plan.xb
+            x = index % plan.xb
+            scale = weight[at * group + c]
+            row = pl.multiple_of(index * plan.yb, plan.yb)
+            spot = pl.multiple_of(x * plan.yb, plan.yb)
+            for first in range(0, plan.cells, lanes):
+                cut = pl.ds(first, lanes)
+                slope = gelu_slope(pre[0, 0, c, x, :, cut].astype(F32))
+                incoming = values[pl.ds(row, plan.yb), cut] + skip[c, x, :, cut].astype(F32)
+                value = (incoming * slope).astype(BF16)
+                fields_ref = wide[1]
+                fields_ref[pl.ds(row, plan.yb), cut] = value
+                projected[pl.ds(spot, plan.yb), cut] += value.astype(F32) * scale
+            return carry
+
+        lax.fori_loop(0, group * plan.xb, line, 0)
+        plane_in(plan, at, wide[1][...], t_plane, wide[0], over_a)
+
+    @pl.when(jnp.logical_and(step >= 2, step <= groups + 1))
+    def _():
+        x_in(plan, step - 2, t_x, over_a, over_b)
+
+    @pl.when(step >= 3)
+    def _():
+        y_in(plan, step - 3, t_y, over_b, spectrum)
+
+    @pl.when(step == groups + 2)
+    def _():
+        for each in (back_a, back_b, over_a, over_b):
+            each.finish(groups)
+
+
+def middle_entry(plan, *refs):
+    middle_kernel(plan, *refs[:13], (refs[13], refs[14]), *refs[15:])
+
+
+def tail_kernel(plan, modes, projected, s_y, s_x, s_plane, result, *scratch):
+    over_a, over_b = exchanges(plan, scratch)
+    greet(plan)
+    y_out(plan, 0, modes[0], s_y, over_b)
+    x_out(plan, 0, s_x, over_b, over_a)
+    result[...] = projected[...] + plane_out(plan, 0, 1, s_plane, over_a)
+    over_a.finish(1)
+    over_b.finish(1)
+
+
+def whole():
+    return pl.BlockSpec(memory_space=pltpu.VMEM, pipeline_mode=pl.Buffered(1))
+
+
+VMEM_LIMIT = 62 * 1024 * 1024
+
+
+def forward_call(plan, layer, cotangent, pre_activations, tables, mix):
+    groups, group = plan.groups, plan.group
+    field = (plan.xb, plan.yb, plan.cells)
+
+    def at_group(step):
+        return jnp.minimum(step, groups - 1)
+
+    return pl.pallas_call(
+        functools.partial(forward_kernel, plan),
+        grid=(groups + 2,),
+        in_specs=[
+            pl.BlockSpec((1, group) + field, lambda s: (0, at_group(s), 0, 0, 0)),
+            pl.BlockSpec((1, 1, group) + field, lambda s: (layer, 0, at_group(s), 0, 0, 0)),
+            whole(),
+            whole(),
+            whole(),
+            whole(),
+        ],
+        out_specs=[
+            pl.BlockSpec(
+                (plan.channels, plan.xb // 2, plan.yb, plan.cells),
+                lambda s: (0, jnp.clip(s - groups, 0, 1), 0, 0),
+            ),
+            pl.BlockSpec(
+                (1, plan.tall, plan.modes), lambda s: (jnp.clip(s - 2, 0, groups - 1), 0, 0)
+            ),
+        ],
+        out_shape=[
+            jax.ShapeDtypeStruct((plan.channels,) + field, BF16),
+            jax.ShapeDtypeStruct((groups, plan.tall, plan.modes), BF16),
+        ],
+        scratch_shapes=[
+            pltpu.VMEM((plan.channels,) + field, BF16),
+            pltpu.VMEM((2 * KZ * KT, group * plan.spots), F32),
+        ]
+        + exchange_scratch(plan, groups, plan.tall),
+        compiler_params=pltpu.CompilerParams(
+            collective_id=1, has_side_effects=True, vmem_limit_bytes=VMEM_LIMIT
+        ),
+        name="forward",
+    )(cotangent, pre_activations, tables["plane_in"], tables["x_in"], tables["y_in"], mix)
+
+
+def middle_call(plan, layer, modes, skip, pre_activations, weight, tables):
+    groups, group = plan.groups, plan.group
+    field = (plan.xb, plan.yb, plan.cells)
+
+    def at_group(step):
+        return jnp.clip(step - 1, 0, groups - 1)
+
+    names = ("plane_in", "x_in", "y_in", "y_out", "x_out", "plane_out")
+    return pl.pallas_call(
+        functools.partial(middle_entry, plan),
+        grid=(groups + 3,),
+        in_specs=[
+            whole(),
+            pl.BlockSpec((group,) + field, lambda s: (at_group(s), 0, 0, 0)),
+            pl.BlockSpec((1, 1, group) + field, lambda s: (layer, 0, at_group(s), 0, 0, 0)),
+            pl.BlockSpec(memory_space=pltpu.SMEM),
+        ]
+        + [whole()] * len(names),
+        out_specs=[
+            pl.BlockSpec(
+                (1, plan.tall, plan.modes), lambda s: (jnp.clip(s - 3, 0, groups - 1), 0, 0)
+            ),
+            pl.BlockSpec((plan.spots, plan.cells), lambda s: (0, 0)),
+        ],
+        out_shape=[
+            jax.ShapeDtypeStruct((groups, plan.tall, plan.modes), BF16),
+            jax.ShapeDtypeStruct((plan.spots, plan.cells), F32),
+        ],
+        scratch_shapes=[
+            pltpu.VMEM((group * plan.spots, plan.cells), F32),
+            pltpu.VMEM((2 * KZ * KT, group * plan.spots), F32),
+            pltpu.VMEM((group * plan.spots, plan.cells), BF16),
+        ]
+        + exchange_scratch(plan, groups, plan.tall)
+        + exchange_scratch(plan, groups, plan.tall),
+        compiler_params=pltpu.CompilerParams(
+            collective_id=2, has_side_effects=True, vmem_limit_bytes=VMEM_LIMIT
+        ),
+        name="middle",
+    )(modes, skip, pre_activations, weight, *[tables[name] for name in names])
+
+
+def tail_call(plan, modes, projected, tables):
+    tall = modes.shape[1]
+    names = ("y_out", "x_out", "plane_out")
+    return pl.pallas_call(
+        functools.partial(tail_kernel, plan),
+        in_specs=[pl.BlockSpec(memory_space=pltpu.VMEM)] * 5,
+        out_specs=pl.BlockSpec(memory_space=pltpu.VMEM),
+        out_shape=jax.ShapeDtypeStruct((plan.spots, plan.cells), F32),
+        scratch_shapes=exchange_scratch(plan, 1, tall),
+        compiler_params=pltpu.CompilerParams(
+            collective_id=3, has_side_effects=True, vmem_limit_bytes=VMEM_LIMIT
+        ),
+        name="tail",
+    )(modes, projected, *[tables[name] for name in names])
+
+
+def by_frequency(plan, spectrum):
+    gridded = spectrum.reshape(plan.channels, plan.mb, 2, plan.kb, KY)
+    turned = gridded.transpose(2, 0, 3, 1, 4)
+    return turned.reshape(2, plan.channels, plan.kb, plan.mb * KY).astype(F32)
+
+
+def per_device(plan, cotangent, pre_activations, spectral_weights, skip_weights, lift_weights):
+    tables = dense_tables(plan)
+    mix = jnp.kron(skip_weights[1].T, jnp.eye(plan.yb, dtype=BF16))
+    skip, spectrum = forward_call(plan, 1, cotangent, pre_activations, tables, mix)
+
+    def mixing(values, matrix):
+        return jnp.sum(values[:, None] * matrix.astype(F32), 0)
+
+    spectrum = by_frequency(plan, spectrum)
+    upper = spectral_weights[1]
+    real = mixing(spectrum[0], upper[0]) + mixing(spectrum[1], upper[1])
+    imag = mixing(spectrum[1], upper[0]) - mixing(spectrum[0], upper[1])
+    modes = jnp.stack([real, imag]).astype(BF16)
+    modes = modes.reshape(2, plan.channels, plan.kb, plan.mb, KY).transpose(1, 3, 0, 2, 4)
+    modes = modes.reshape(plan.groups, plan.tall, plan.modes)
+    weight = jnp.sum(skip_weights[0].astype(F32) * lift_weights[None, :], 1)
+    spectrum, projected = middle_call(plan, 0, modes, skip, pre_activations, weight, tables)
+
+    spectrum = by_frequency(plan, spectrum)
+    lifted = lift_weights[None, None, :, None, None]
+    lower = jnp.sum(spectral_weights[0].astype(F32) * lifted, 2)
+    real = jnp.sum(spectrum[0] * lower[0] + spectrum[1] * lower[1], 0)
+    imag = jnp.sum(spectrum[1] * lower[0] - spectrum[0] * lower[1], 0)
+    modes = jnp.stack([real, imag]).reshape(2, plan.kb, plan.mb, KY).transpose(2, 0, 1, 3)
+    modes = modes.reshape(1, plan.mb, plan.modes).astype(BF16)
+    modes = jnp.pad(modes, ((0, 0), (0, -plan.mb % 16), (0, 0)))
+    result = tail_call(plan, modes, projected, tables)
+    return result.reshape(1, plan.xb, plan.yb, plan.cells)
+
+
 def solution(mesh):
+    def step(cotangent, pre_activations, spectral_weights, skip_weights, lift_weights):
+        plan = Plan(mesh, cotangent.shape[1])
+        layers, samples = pre_activations.shape[:2]
+        if layers == 2 and samples == 1 and plan.fits():
+            body = functools.partial(per_device, plan)
+        else:
+            body = per_device_plain
+        return body(cotangent, pre_activations, spectral_weights, skip_weights, lift_weights)
+
     return jax.shard_map(
-        per_device,
+        step,
         mesh=mesh,
         in_specs=(
             P(None, None, "aa", "ba", None),

time: 760 us -> 261 us (0.34); the launches traced: 751 us -> 260 us
  local copies, waits for them, and re-layouts: 366 us -> 60.3 us
  Pallas kernels: 0 us -> 178 us
  matrix products: 169 us -> 0 us
  blocking collectives: 158 us -> 0 us
  other arithmetic: 41.7 us -> 21.2 us
  starting transfers between devices: 8.86 us -> 0 us
    unnamed x49 -> x5, local copies, waits for them, and re-layouts: 241 us -> 2.31 us
    pallas_call x0 -> x3, Pallas kernels: none -> 178 us  [the longest x1 101 us: middle_call(): pl.pallas_call(functools.partial(middle_entry, plan), grid=(groups + 3,),...]
    dot_general x13 -> x0, matrix products: 169 us -> none  [the longest x10 147 us: rounded_product(): jnp.einsum(pattern, values, jnp.asarray(table, jnp.bfloat16), preferred_e...]
    all_to_all x6 -> x0, blocking collectives: 158 us -> none  [exchange(): return lax.all_to_all(values, axis, split_axis=0, concat_axis=0, tiled=True)]
    convert_element_type x9 -> x6, local copies, waits for them, and re-layouts: 55.2 us -> 12.6 us  [the longest x4 12.3 us: by_frequency(): return turned.reshape(2, plan.channels, plan.kb, plan.mb * KY).astype(F32)]
    dot_general x2 -> x0, other arithmetic: 27.4 us -> none  [mixing(): jnp.einsum('bokr,oikr->bikr', values, matrix, preferred_element_type=jnp....]
    reduce_sum x2 -> x4, other arithmetic: 1.08 us -> 20.2 us  [the longest x1 13.3 us: per_device(): lower = jnp.sum(spectral_weights[0].astype(F32) * lifted, 2)]
    another operation x8 -> x2, local copies, waits for them, and re-layouts: 16.9 us -> 0.22 us  [per_device(): jnp.stack([real, imag]).reshape(2, plan.kb, plan.mb, KY)]
  transfers between devices with their start and end apart: 2 -> 0, of which waited for: 1 -> 0; matrix products, arithmetic and copies ran while one was open for 9% -> 0% of each run, Pallas kernels for 0% -> 0%
where the time goes in v1:
time: 261 us; the launch traced here: 260 us
  Pallas kernels  178 us (68%)
  local copies, waits for them, and re-layouts  60.3 us (23%)
  other arithmetic  21.2 us (8%)
    pallas_call x1, Pallas kernels, middle_call(): pl.pallas_call(functools.partial(middle_entry, plan), grid=(groups + 3,),...  101 us
    pallas_call x1, Pallas kernels, forward_call(): pl.pallas_call(functools.partial(forward_kernel, plan), grid=(groups + 2,...  59 us
    slice x2, local copies, waits for them, and re-layouts, per_device(): real = mixing(spectrum[0], upper[0]) + mixing(spectrum[1], upper[1])  19 us
    pallas_call x1, Pallas kernels, tail_call(): pl.pallas_call(functools.partial(tail_kernel, plan), in_specs=[pl.BlockSp...  18 us
    reduce_sum x1, other arithmetic, per_device(): lower = jnp.sum(spectral_weights[0].astype(F32) * lifted, 2)  13.3 us
    convert_element_type x4, local copies, waits for them, and re-layouts, by_frequency(): return turned.reshape(2, plan.channels, plan.kb, plan.mb * KY).astype(F32)  12.3 us
    slice x5, local copies, waits for them, and re-layouts, per_device(): real = jnp.sum(spectrum[0] * lower[0] + spectrum[1] * lower[1], 0)  10 us
    mul x4, local copies, waits for them, and re-layouts, mixing(): return jnp.sum(values[:, None] * matrix.astype(F32), 0)  6.86 us

profile of v1, /device:TPU:0, one launch (start us, length us, event | category | flops | bytes accessed | tf_op | source)
XLA Modules:
  0.0 260.2 jit_solution(6963158082046984736)
XLA Ops:
  1.1 1.8 mul.91.mix
  3.0 59.0 %forward.1 = (bf16[20,8,16,2048]{3,2,1,0:T(8,128)(2,1)}, bf16[5,144,288]{2,1,0:T(8,128)(2,1)}) custom-call(bf16[1,20,8,16,2048]{4,3,2,1,0:T(8,128)(2,1)} %cotangent.1, bf16[2,1,20,8,16,2048]{5,4,3,2,1,0:T(8,128)(2,1)} %refs_2_.1, bf16[576,2048]{1,0:T(8,128)(2,1)} %constant.17.clone.t_plane.refs_4_, bf16[2048,1024]{1,0:T(8,128)(2,1)} %constant.18.clone.t_x.refs_5_, ...), custom_call_target="tpu_custom_call" | custom-call | tf_op jit(solution)/shard_map/forward/pallas_call | solution.py:525
  62.0 2.8 %copy.16 = f32[5,144,288]{1,0,2:T(8,128)} copy(bf16[5,144,288]{2,1,0:T(8,128)(2,1)} %get-tuple-element.9) | data formatting | bytes 1244160 | tf_op jit(solution)/shard_map/convert_element_type | solution.py:622
  64.8 3.4 %reshape.126 = f32[20,36,2,6,24]{1,0,4,3,2:T(8,128)S(1)} reshape(f32[5,144,288]{1,0,2:T(8,128)} %copy.16) | data formatting | bytes 1658880 | tf_op jit(solution)/shard_map/convert_element_type | solution.py:622
  68.2 2.1 fusion.9
  70.3 2.2 copy.31
  73.3 2.2 copy.32
  75.5 1.6 reshape.129
  77.2 16.9 %fusion.7 = (bf16[1,1,20,20,6,864]{5,1,4,3,2,0:T(2,128)(2,1)S(1)}, bf16[1,1,20,20,6,864]{5,1,4,3,2,0:T(2,128)(2,1)S(1)}) fusion(bf16[2,2,20,20,6,864]{5,1,4,3,2,0:T(2,128)(2,1)} %param.13), kind=kLoop, calls=%fused_computation.24 | loop fusion | bytes 16588800 | tf_op jit(solution)/shard_map/slice | solution.py:635
  94.0 4.8 %fusion.1 = (f32[20,6,864]{2,0,1:T(8,128)S(1)}, f32[20,6,864]{2,0,1:T(8,128)S(1)}, f32[20,6,864]{2,0,1:T(8,128)S(1)}, f32[20,6,864]{2,0,1:T(8,128)S(1)}) fusion(f32[20,6,864]{2,1,0:T(8,128)S(1)} %reshape.128, bf16[1,1,20,20,6,864]{5,1,4,3,2,0:T(2,128)(2,1)S(1)} %get-tuple-element.22, f32[20,6,864]{2,1,0:T(8,128)S(1)} %copy-done, ...), kind=kLoop, calls=%fused_computation.6 | loop fusion | flops 20321280 | bytes 10782720 | tf_op jit(solution)/shard_map/reduce_sum | solution.py:631
  101.4 1.0 copy.33
  102.4 3.2 %reshape.130.refs_0_ = bf16[5,144,288]{2,1,0:T(8,128)(2,1)} reshape(bf16[20,36,2,6,24]{4,3,2,1,0:T(8,128)(2,1)S(1)} %copy.33) | data formatting | bytes 829440 | tf_op jit(solution)/shard_map/reshape | solution.py:639
  106.3 101.4 %middle.1 = (bf16[5,144,288]{2,1,0:T(8,128)(2,1)}, f32[128,2048]{1,0:T(8,128)}) custom-call(bf16[5,144,288]{2,1,0:T(8,128)(2,1)} %reshape.130.refs_0_, bf16[20,8,16,2048]{3,2,1,0:T(8,128)(2,1)} %get-tuple-element.10.refs_1_, bf16[2,1,20,8,16,2048]{5,4,3,2,1,0:T(8,128)(2,1)} %refs_2_.1, f32[20]{0:T(128)} %fusion.5.refs_3_, ...), custom_call_target="tpu_custom_call" | custom-call | tf_op jit(solution)/shard_map/middle/pallas_call | solution.py:569
  207.8 2.8 %copy.26 = f32[5,144,288]{1,0,2:T(8,128)} copy(bf16[5,144,288]{2,1,0:T(8,128)(2,1)} %get-tuple-element.11) | data formatting | bytes 1244160 | tf_op jit(solution)/shard_map/convert_element_type | solution.py:622
  210.5 3.4 %reshape.127 = f32[20,36,2,6,24]{1,0,4,3,2:T(8,128)S(1)} reshape(f32[5,144,288]{1,0,2:T(8,128)} %copy.26) | data formatting | bytes 1658880 | tf_op jit(solution)/shard_map/convert_element_type | solution.py:622
  213.9 2.0 fusion.8
  215.9 2.4 copy.27
  218.3 1.7 slice.61
  220.1 2.2 copy.28
  222.3 1.7 slice.65
  224.0 13.3 %fusion = f32[2,20,6,864]{3,0,2,1:T(2,128)S(1)} fusion(f32[20]{0:T(128)S(1)} %copy-done.1, bf16[2,2,20,20,6,864]{5,1,4,3,2,0:T(2,128)(2,1)} %param.13), kind=kLoop, calls=%fused_computation.1 | loop fusion | flops 12234240 | bytes 9123920 | tf_op jit(solution)/shard_map/reduce_sum | solution.py:645
  237.3 1.4 add_reduce_fusion
  239.9 18.0 %tail.1 = f32[128,2048]{1,0:T(8,128)} custom-call(bf16[1,48,288]{2,1,0:T(8,128)(2,1)} %pad.4.modes, f32[128,2048]{1,0:T(8,128)} %get-tuple-element.12.projected, bf16[288,1024]{1,0:T(8,128)(2,1)} %constant.20.clone.refs_7_.s_y, bf16[1024,2048]{1,0:T(8,128)(2,1)} %constant.21.clone.refs_8_.s_x, bf16[576,2048]{1,0:T(8,128)(2,1)} %constant.22.clone.refs_9_.s_plane), custom_call_target="tpu_custom_call" | custom-call | tf_op jit(solution)/shard_map/tail/pallas_call | solution.py:606
  257.9 2.3 copy.56
  (20 shorter events, 6.4 us)
Async XLA Ops:
  77.2 16.9 %copy-start = (f32[20,6,864]{2,1,0:T(8,128)S(1)}, f32[20,6,864]{2,1,0:T(8,128)}, u32[]{:S(2)}) copy-start(f32[20,6,864]{2,1,0:T(8,128)} %reshape.129) | copy-start | bytes 1244164
  101.4 4.2 %copy-start.1 = (f32[20]{0:T(128)S(1)}, f32[20]{0:T(128)}, u32[]{:S(2)}) copy-start(f32[20]{0:T(128)} %param.15) | copy-start | bytes 244

commit v2 on v1

--- a/solution.py
+++ b/solution.py
@@ -180,7 +180,9 @@
         self.tall = self.group * self.mb
         self.half = 128
         self.kpad = self.half // self.yb
-        self.modes = 2 * self.kb * KY
+        self.modes = self.kb * KY
+        self.room = -(-self.modes // 128) * 128
+        self.lines = self.mb * KY
 
     def fits(self):
         return (
@@ -219,10 +221,12 @@
     tables["x_in"] = wide.reshape(rows * 2 * plan.spots, columns * 2 * plan.half)
     part = real_form(along_y.conj().T).reshape(2, columns, plan.yb, 2, KY)
     wide = np.einsum("pbyqj,kl->bplyqkj", part, eye_k)
-    tables["y_in"] = wide.reshape(columns * 2 * plan.half, plan.modes)
+    wide = wide.reshape(columns * 2 * plan.half, 2, plan.modes)
+    wide = np.pad(wide, ((0, 0), (0, 0), (0, plan.room - plan.modes)))
+    tables["y_in"] = wide.reshape(columns * 2 * plan.half, 2 * plan.room)
     part = (real_form(along_y) / NY).reshape(2, KY, 2, columns, plan.yb)
     wide = np.einsum("pjqhy,kl->pkjhqly", part, eye_k)
-    tables["y_out"] = wide.reshape(plan.modes, columns * 2 * plan.half)
+    tables["y_out"] = wide.reshape(2, plan.modes, columns * 2 * plan.half)
     part = (real_form(along_x) / NX).reshape(2, columns, plan.kb, 2, rows, plan.xb)
     wide = np.einsum("pbkqnx,yw,kl->bplynqxw", part, eye_y, eye_k)
     tables["x_out"] = wide.reshape(columns * 2 * plan.half, rows * 2 * plan.spots)
@@ -334,17 +338,87 @@
     over_b.start(group)
 
 
-def y_in(plan, group, table, over_b, spectrum):
+def y_in(plan, group, table, over_b, sheet, real_first, imag_first):
     over_b.arrive(group)
     result = product(joined(over_b.into, group, plan.columns), table[...])
-    spectrum[0] = result.astype(BF16)
-
-
-def y_out(plan, group, values, table, over_b):
-    result = product(values, table[...]).astype(BF16)
+    mb = plan.mb
+    for c in range(plan.group):
+        for part in range(2):
+            lane = part * plan.room
+            row = (2 * c + part) * mb
+            for half in range(plan.room // 128):
+                first = lane + 128 * half
+                piece = result[c * mb : (c + 1) * mb, first : first + 128]
+                sheet[half, row : row + mb] = piece
+    count = 2 * plan.group
+    lines = []
+    for m in range(mb):
+        row = pl.ds(m, count, stride=mb)
+        lines.append(jnp.concatenate([sheet[h, row, :] for h in range(plan.room // 128)], 1))
+    for k in range(plan.kb):
+        turned = jnp.concatenate([line[:, k * KY : (k + 1) * KY] for line in lines], 1)
+        for c in range(plan.group):
+            real = turned[2 * c : 2 * c + 1]
+            imag = turned[2 * c + 1 : 2 * c + 2]
+            real_first[c, k] = jnp.concatenate([real, imag], 0)
+            imag_first[c, k] = jnp.concatenate([imag, -real], 0)
+
+
+def mix_in(plan, weights, real_first, imag_first, real_sum, imag_sum):
+    for c in range(plan.group):
+        for k in range(plan.kb):
+            first = real_first[c, k]
+            second = imag_first[c, k]
+
+            def add(i, carry):
+                matrix = weights[0, c, i, k].astype(F32)
+                real_sum[i, k] += matrix * first
+                imag_sum[i, k] += matrix * second
+                return carry
+
+            lax.fori_loop(0, plan.channels, add, 0, unroll=10)
+
+
+def fold_in(plan, group, weights, lift, folded):
+    for c in range(plan.group):
+
+        def line(k, carry):
+            total = weights[0, c, 0, k].astype(F32) * lift[0]
+            for i in range(1, plan.channels):
+                total = total + weights[0, c, i, k].astype(F32) * lift[i]
+            folded[group * plan.group + c, k] = total
+            return carry
+
+        lax.fori_loop(0, plan.kb, line, 0)
+
+
+def by_row(plan, rows, sheet):
+    count = rows[0].shape[0]
+    for m in range(plan.mb):
+        pieces = [row[:, m * KY : (m + 1) * KY] for row in rows]
+        if plan.room > plan.modes:
+            pieces.append(jnp.zeros((count, plan.room - plan.modes), F32))
+        line = jnp.concatenate(pieces, 1)
+        for half in range(plan.room // 128):
+            row = pl.ds(m, count, stride=plan.mb)
+            sheet[half, row, :] = line[:, half * 128 : (half + 1) * 128]
+
+
+def sheet_rows(plan, sheet, first, last):
+    halves = [sheet[half, first:last] for half in range(plan.room // 128)]
+    return jnp.concatenate(halves, 1)[:, : plan.modes].astype(BF16)
+
+
+def y_out(plan, group, parts, table, over_b):
+    result = (product(parts[0], table[0]) + product(parts[1], table[1])).astype(BF16)
     width = 2 * plan.half
+    tall = result.shape[0]
     for owner in range(plan.columns):
-        over_b.out[group, owner] = result[:, owner * width : (owner + 1) * width]
+        cut = result[:, owner * width : (owner + 1) * width]
+        if tall < over_b.out.shape[2]:
+            over_b.out[group, owner, :tall] = cut
+        else:
+            over_b.out[group, owner] = cut
     over_b.start(group)
 
 
@@ -378,7 +452,10 @@
     return product(values, table[...], ((0,), (0,)))
 
 
-def forward_kernel(plan, cotangent, pre, t_plane, t_x, t_y, mix, skip, spectrum, field, wide, *scratch):
+def forward_kernel(
+    plan, cotangent, pre, weights, t_plane, t_x, t_y, mix, skip, modes,
+    field, wide, sheet, real_first, imag_first, real_sum, imag_sum, *scratch,
+):
     step = pl.program_id(0)
     over_a, over_b = exchanges(plan, scratch)
     groups, group = plan.groups, plan.group
@@ -387,6 +464,8 @@
     @pl.when(step == 0)
     def _():
         greet(plan)
+        real_sum[...] = jnp.zeros_like(real_sum)
+        imag_sum[...] = jnp.zeros_like(imag_sum)
 
     @pl.when(step < groups)
     def _():
@@ -423,22 +502,39 @@
 
     @pl.when(step >= 2)
     def _():
-        y_in(plan, step - 2, t_y, over_b, spectrum)
+        y_in(plan, step - 2, t_y, over_b, sheet, real_first, imag_first)
+        mix_in(plan, weights, real_first, imag_first, real_sum, imag_sum)
 
     @pl.when(step == groups + 1)
     def _():
+        def turn(index, carry):
+            rows = []
+            for k in range(plan.kb):
+                row = []
+                for total in (real_sum, imag_sum):
+                    for c in range(group):
+                        both = total[index * group + c, k]
+                        row.append(both[:1] + both[1:])
+                rows.append(jnp.concatenate(row, 0))
+            by_row(plan, rows, sheet)
+            modes[index] = sheet_rows(plan, sheet, 0, 2 * plan.tall)
+            return carry
+
+        lax.fori_loop(0, groups, turn, 0)
         over_a.finish(groups)
         over_b.finish(groups)
 
 
 def middle_kernel(
-    plan, modes, skip, pre, weight, t_plane, t_x, t_y, s_y, s_x, s_plane,
-    spectrum, projected, values, wide, *scratch,
+    plan, modes, skip, pre, weights, weight, lift, t_plane, t_x, t_y, s_y, s_x, s_plane,
+    result, values, wide, field, sheet, real_first, imag_first, folded, real_sum, imag_sum,
+    *scratch,
 ):
     step = pl.program_id(0)
     back_a, back_b = exchanges(plan, scratch[:8])
-    over_a, over_b = exchanges(plan, scratch[8:])
-    groups, group = plan.groups, plan.group
+    over_a, over_b = exchanges(plan, scratch[8:16])
+    last_a, last_b = exchanges(plan, scratch[16:])
+    groups, group, tall = plan.groups, plan.group, plan.tall
     lanes = 512
 
     @pl.when(step == 0)
@@ -446,14 +542,17 @@
         greet(plan)
 
         def send(index, carry):
-            y_out(plan, index, modes[index], s_y, back_b)
+            y_out(plan, index, (modes[index, :tall], modes[index, tall:]), s_y, back_b)
             return carry
 
         lax.fori_loop(0, groups, send, 0)
-        projected[...] = jnp.zeros_like(projected)
+        result[...] = jnp.zeros_like(result)
+        real_sum[...] = jnp.zeros_like(real_sum)
+        imag_sum[...] = jnp.zeros_like(imag_sum)
 
     @pl.when(step < groups)
     def _():
+        fold_in(plan, step, weights, lift, folded)
         x_out(plan, step, s_x, back_b, back_a)
 
     @pl.when(jnp.logical_and(step >= 1, step <= groups))
@@ -472,13 +571,12 @@
                 slope = gelu_slope(pre[0, 0, c, x, :, cut].astype(F32))
                 incoming = values[pl.ds(row, plan.yb), cut] + skip[c, x, :, cut].astype(F32)
                 value = (incoming * slope).astype(BF16)
-                fields_ref = wide[1]
-                fields_ref[pl.ds(row, plan.yb), cut] = value
-                projected[pl.ds(spot, plan.yb), cut] += value.astype(F32) * scale
+                field[pl.ds(row, plan.yb), cut] = value
+                result[pl.ds(spot, plan.yb), cut] += value.astype(F32) * scale
             return carry
 
         lax.fori_loop(0, group * plan.xb, line, 0)
-        plane_in(plan, at, wide[1][...], t_plane, wide[0], over_a)
+        plane_in(plan, at, field[...], t_plane, wide, over_a)
 
     @pl.when(jnp.logical_and(step >= 2, step <= groups + 1))
     def _():
@@ -486,26 +584,29 @@
 
     @pl.when(step >= 3)
     def _():
-        y_in(plan, step - 3, t_y, over_b, spectrum)
+        at = step - 3
+        y_in(plan, at, t_y, over_b, sheet, real_first, imag_first)
+        for c in range(group):
+            matrix = folded[at * group + c]
+            real_sum[...] += matrix * real_first[c]
+            imag_sum[...] += matrix * imag_first[c]
 
     @pl.when(step == groups + 2)
     def _():
+        rows = []
+        for k in range(plan.kb):
+            row = [total[k, :1] + total[k, 1:] for total in (real_sum, imag_sum)]
+            rows.append(jnp.concatenate(row, 0))
+        by_row(plan, rows, sheet)
+        mb = plan.mb
+        parts = [sheet_rows(plan, sheet, p * mb, (p + 1) * mb) for p in range(2)]
+        y_out(plan, 0, parts, s_y, last_b)
+        x_out(plan, 0, s_x, last_b, last_a)
+        result[...] += plane_out(plan, 0, 1, s_plane, last_a)
         for each in (back_a, back_b, over_a, over_b):
             each.finish(groups)
-
-
-def middle_entry(plan, *refs):
-    middle_kernel(plan, *refs[:13], (refs[13], refs[14]), *refs[15:])
-
-
-def tail_kernel(plan, modes, projected, s_y, s_x, s_plane, result, *scratch):
-    over_a, over_b = exchanges(plan, scratch)
-    greet(plan)
-    y_out(plan, 0, modes[0], s_y, over_b)
-    x_out(plan, 0, s_x, over_b, over_a)
-    result[...] = projected[...] + plane_out(plan, 0, 1, s_plane, over_a)
-    over_a.finish(1)
-    over_b.finish(1)
+        for each in (last_a, last_b):
+            each.finish(1)
 
 
 def whole():
@@ -515,9 +616,25 @@
 VMEM_LIMIT = 62 * 1024 * 1024
 
 
-def forward_call(plan, layer, cotangent, pre_activations, tables, mix):
+def weight_spec(plan, layer, first):
+    block = (1, plan.group, plan.channels, plan.kb, 2, plan.lines)
+    last = plan.groups - 1
+    return pl.BlockSpec(block, lambda s: (layer, jnp.clip(s - first, 0, last), 0, 0, 0, 0))
+
+
+def mixing_scratch(plan):
+    line = (2, plan.lines)
+    return [
+        pltpu.VMEM((plan.room // 128, 2 * plan.tall, 128), F32),
+        pltpu.VMEM((plan.group, plan.kb) + line, F32),
+        pltpu.VMEM((plan.group, plan.kb) + line, F32),
+    ]
+
+
+def forward_call(plan, layer, cotangent, pre_activations, weights, tables, mix):
     groups, group = plan.groups, plan.group
     field = (plan.xb, plan.yb, plan.cells)
+    sums = (plan.channels, plan.kb, 2, plan.lines)
 
     def at_group(step):
         return jnp.minimum(step, groups - 1)
@@ -528,6 +645,7 @@
         in_specs=[
             pl.BlockSpec((1, group) + field, lambda s: (0, at_group(s), 0, 0, 0)),
             pl.BlockSpec((1, 1, group) + field, lambda s: (layer, 0, at_group(s), 0, 0, 0)),
+            weight_spec(plan, layer, 2),
             whole(),
             whole(),
             whole(),
@@ -538,117 +656,76 @@
                 (plan.channels, plan.xb // 2, plan.yb, plan.cells),
                 lambda s: (0, jnp.clip(s - groups, 0, 1), 0, 0),
             ),
-            pl.BlockSpec(
-                (1, plan.tall, plan.modes), lambda s: (jnp.clip(s - 2, 0, groups - 1), 0, 0)
-            ),
+            pl.BlockSpec((groups, 2 * plan.tall, plan.modes), lambda s: (0, 0, 0)),
         ],
         out_shape=[
             jax.ShapeDtypeStruct((plan.channels,) + field, BF16),
-            jax.ShapeDtypeStruct((groups, plan.tall, plan.modes), BF16),
+            jax.ShapeDtypeStruct((groups, 2 * plan.tall, plan.modes), BF16),
         ],
         scratch_shapes=[
             pltpu.VMEM((plan.channels,) + field, BF16),
             pltpu.VMEM((2 * KZ * KT, group * plan.spots), F32),
         ]
+        + mixing_scratch(plan)
+        + [pltpu.VMEM(sums, F32), pltpu.VMEM(sums, F32)]
         + exchange_scratch(plan, groups, plan.tall),
         compiler_params=pltpu.CompilerParams(
             collective_id=1, has_side_effects=True, vmem_limit_bytes=VMEM_LIMIT
         ),
         name="forward",
-    )(cotangent, pre_activations, tables["plane_in"], tables["x_in"], tables["y_in"], mix)
-
-
-def middle_call(plan, layer, modes, skip, pre_activations, weight, tables):
+    )(cotangent, pre_activations, weights, tables["plane_in"], tables["x_in"], tables["y_in"], mix)
+
+
+def middle_call(plan, layer, modes, skip, pre_activations, weights, weight, lift, tables):
     groups, group = plan.groups, plan.group
     field = (plan.xb, plan.yb, plan.cells)
+    sums = (plan.kb, 2, plan.lines)
 
     def at_group(step):
         return jnp.clip(step - 1, 0, groups - 1)
 
     names = ("plane_in", "x_in", "y_in", "y_out", "x_out", "plane_out")
     return pl.pallas_call(
-        functools.partial(middle_entry, plan),
+        functools.partial(middle_kernel, plan),
         grid=(groups + 3,),
         in_specs=[
             whole(),
             pl.BlockSpec((group,) + field, lambda s: (at_group(s), 0, 0, 0)),
             pl.BlockSpec((1, 1, group) + field, lambda s: (layer, 0, at_group(s), 0, 0, 0)),
+            weight_spec(plan, layer, 0),
+            pl.BlockSpec(memory_space=pltpu.SMEM),
             pl.BlockSpec(memory_space=pltpu.SMEM),
         ]
         + [whole()] * len(names),
-        out_specs=[
-            pl.BlockSpec(
-                (1, plan.tall, plan.modes), lambda s: (jnp.clip(s - 3, 0, groups - 1), 0, 0)
-            ),
-            pl.BlockSpec((plan.spots, plan.cells), lambda s: (0, 0)),
-        ],
-        out_shape=[
-            jax.ShapeDtypeStruct((groups, plan.tall, plan.modes), BF16),
-            jax.ShapeDtypeStruct((plan.spots, plan.cells), F32),
-        ],
+        out_specs=pl.BlockSpec((plan.spots, plan.cells), lambda s: (0, 0)),
+        out_shape=jax.ShapeDtypeStruct((plan.spots, plan.cells), F32),
         scratch_shapes=[
             pltpu.VMEM((group * plan.spots, plan.cells), F32),
             pltpu.VMEM((2 * KZ * KT, group * plan.spots), F32),
             pltpu.VMEM((group * plan.spots, plan.cells), BF16),
         ]
+        + mixing_scratch(plan)
+        + [pltpu.VMEM((plan.channels,) + sums, F32)]
+        + [pltpu.VMEM(sums, F32), pltpu.VMEM(sums, F32)]
         + exchange_scratch(plan, groups, plan.tall)
-        + exchange_scratch(plan, groups, plan.tall),
+        + exchange_scratch(plan, groups, plan.tall)
+        + exchange_scratch(plan, 1, -(-plan.mb // 16) * 16),
         compiler_params=pltpu.CompilerParams(
             collective_id=2, has_side_effects=True, vmem_limit_bytes=VMEM_LIMIT
         ),
         name="middle",
-    )(modes, skip, pre_activations, weight, *[tables[name] for name in names])
-
-
-def tail_call(plan, modes, projected, tables):
-    tall = modes.shape[1]
-    names = ("y_out", "x_out", "plane_out")
-    return pl.pallas_call(
-        functools.partial(tail_kernel, plan),
-        in_specs=[pl.BlockSpec(memory_space=pltpu.VMEM)] * 5,
-        out_specs=pl.BlockSpec(memory_space=pltpu.VMEM),
-        out_shape=jax.ShapeDtypeStruct((plan.spots, plan.cells), F32),
-        scratch_shapes=exchange_scratch(plan, 1, tall),
-        compiler_params=pltpu.CompilerParams(
-            collective_id=3, has_side_effects=True, vmem_limit_bytes=VMEM_LIMIT
-        ),
-        name="tail",
-    )(modes, projected, *[tables[name] for name in names])
-
-
-def by_frequency(plan, spectrum):
-    gridded = spectrum.reshape(plan.channels, plan.mb, 2, plan.kb, KY)
-    turned = gridded.transpose(2, 0, 3, 1, 4)
-    return turned.reshape(2, plan.channels, plan.kb, plan.mb * KY).astype(F32)
+    )(modes, skip, pre_activations, weights, weight, lift, *[tables[name] for name in names])
 
 
 def per_device(plan, cotangent, pre_activations, spectral_weights, skip_weights, lift_weights):
     tables = dense_tables(plan)
+    weights = spectral_weights.transpose(0, 2, 3, 4, 1, 5)
     mix = jnp.kron(skip_weights[1].T, jnp.eye(plan.yb, dtype=BF16))
-    skip, spectrum = forward_call(plan, 1, cotangent, pre_activations, tables, mix)
-
-    def mixing(values, matrix):
-        return jnp.sum(values[:, None] * matrix.astype(F32), 0)
-
-    spectrum = by_frequency(plan, spectrum)
-    upper = spectral_weights[1]
-    real = mixing(spectrum[0], upper[0]) + mixing(spectrum[1], upper[1])
-    imag = mixing(spectrum[1], upper[0]) - mixing(spectrum[0], upper[1])
-    modes = jnp.stack([real, imag]).astype(BF16)
-    modes = modes.reshape(2, plan.channels, plan.kb, plan.mb, KY).transpose(1, 3, 0, 2, 4)
-    modes = modes.reshape(plan.groups, plan.tall, plan.modes)
     weight = jnp.sum(skip_weights[0].astype(F32) * lift_weights[None, :], 1)
-    spectrum, projected = middle_call(plan, 0, modes, skip, pre_activations, weight, tables)
-
-    spectrum = by_frequency(plan, spectrum)
-    lifted = lift_weights[None, None, :, None, None]
-    lower = jnp.sum(spectral_weights[0].astype(F32) * lifted, 2)
-    real = jnp.sum(spectrum[0] * lower[0] + spectrum[1] * lower[1], 0)
-    imag = jnp.sum(spectrum[1] * lower[0] - spectrum[0] * lower[1], 0)
-    modes = jnp.stack([real, imag]).reshape(2, plan.kb, plan.mb, KY).transpose(2, 0, 1, 3)
-    modes = modes.reshape(1, plan.mb, plan.modes).astype(BF16)
-    modes = jnp.pad(modes, ((0, 0), (0, -plan.mb % 16), (0, 0)))
-    result = tail_call(plan, modes, projected, tables)
+    skip, modes = forward_call(plan, 1, cotangent, pre_activations, weights, tables, mix)
+    result = middle_call(
+        plan, 0, modes, skip, pre_activations, weights, weight, lift_weights, tables
+    )
     return result.reshape(1, plan.xb, plan.yb, plan.cells)
 
 

time: 261 us -> 187 us (0.72)
  local copies, waits for them, and re-layouts: 60.3 us -> 5.03 us
  other arithmetic: 21.2 us -> 1.54 us
    slice x7 -> x0, local copies, waits for them, and re-layouts: 29 us -> none  [the longest x2 19 us: per_device(): real = mixing(spectrum[0], upper[0]) + mixing(spectrum[1], upper[1])]
    reduce_sum x3 -> x0, other arithmetic: 19.5 us -> none  [the longest x1 13.3 us: per_device(): lower = jnp.sum(spectral_weights[0].astype(F32) * lifted, 2)]
    convert_element_type x6 -> x0, local copies, waits for them, and re-layouts: 12.6 us -> none  [the longest x4 12.3 us: by_frequency(): return turned.reshape(2, plan.channels, plan.kb, plan.mb * KY).astype(F32)]
    mul x4 -> x0, local copies, waits for them, and re-layouts: 6.86 us -> none  [mixing(): return jnp.sum(values[:, None] * matrix.astype(F32), 0)]
    pallas_call x1, Pallas kernels: 59 us -> 64.9 us  [forward_call(): pl.pallas_call(functools.partial(forward_kernel, plan), grid=(groups + 2,...]
    reshape x2 -> x0, local copies, waits for them, and re-layouts: 4.15 us -> none  [per_device(): modes = modes.reshape(plan.groups, plan.tall, plan.modes)]
    pallas_call x2 -> x1, Pallas kernels: 119 us -> 115 us  [middle_call(): pl.pallas_call(functools.partial(middle_kernel, plan), grid=(groups + 3,)...]
where the time goes in v2:
time: 187 us
  Pallas kernels  180 us (96%)
  local copies, waits for them, and re-layouts  5.03 us (3%)
    pallas_call x1, Pallas kernels, middle_call(): pl.pallas_call(functools.partial(middle_kernel, plan), grid=(groups + 3,)...  115 us
    pallas_call x1, Pallas kernels, forward_call(): pl.pallas_call(functools.partial(forward_kernel, plan), grid=(groups + 2,...  64.9 us

profile of v2, /device:TPU:0, one launch (start us, length us, event | category | flops | bytes accessed | tf_op | source)
XLA Modules:
  0.0 186.8 jit_solution(2089116981657192383)
XLA Ops:
  0.0 0.8 fusion.2
  0.8 1.3 fusion.weight
  2.1 0.1 copy.18
  2.3 0.2 broadcast_multiply_fusion
  2.5 1.8 mul.35.mix
  4.3 64.9 %forward.1 = (bf16[20,8,16,2048]{3,2,1,0:T(8,128)(2,1)}, bf16[5,288,144]{2,1,0:T(8,128)(2,1)}) custom-call(bf16[1,20,8,16,2048]{4,3,2,1,0:T(8,128)(2,1)} %cotangent.1, bf16[2,1,20,8,16,2048]{5,4,3,2,1,0:T(8,128)(2,1)} %pre.3, bf16[2,20,20,6,2,864]{5,4,3,2,1,0:T(2,128)(2,1)} %bitcast.11, bf16[576,2048]{1,0:T(8,128)(2,1)} %constant.14.clone.t_plane, ...), custom_call_target="tpu_custom_call" | custom-call | tf_op jit(solution)/shard_map/forward/pallas_call | solution.py:642
  69.2 115.3 %middle.1 = f32[128,2048]{1,0:T(8,128)} custom-call(bf16[5,288,144]{2,1,0:T(8,128)(2,1)} %get-tuple-element.7.modes, bf16[20,8,16,2048]{3,2,1,0:T(8,128)(2,1)} %get-tuple-element.8.skip, bf16[2,1,20,8,16,2048]{5,4,3,2,1,0:T(8,128)(2,1)} %pre.3, bf16[2,20,20,6,2,864]{5,4,3,2,1,0:T(2,128)(2,1)} %bitcast.12, f32[20]{0:T(128)} %fusion.weight, f32[20]{0:T(128)} %lift.1, ...), custom_call_target="tpu_custom_call" | custom-call | tf_op jit(solution)/shard_map/middle/pallas_call | solution.py:688
  184.5 2.3 %copy.23 = f32[1,8,16,2048]{3,2,1,0:T(8,128)} copy(f32[1,8,16,2048]{3,2,1,0:T(8,128)} %bitcast.13) | data formatting | bytes 2097152
  (1 shorter events, 0.0 us)

commit v3 on v2

--- a/solution.py
+++ b/solution.py
@@ -179,7 +179,8 @@
         self.groups = channels // self.group
         self.tall = self.group * self.mb
         self.half = 128
-        self.kpad = self.half // self.yb
+        self.kmain = self.half // (2 * self.yb)
+        self.width = 2 * self.kb * self.yb
         self.modes = self.kb * KY
         self.room = -(-self.modes // 128) * 128
         self.lines = self.mb * KY
@@ -189,7 +190,9 @@
             self.spots == self.half
             and self.half % self.yb == 0
             and self.yb % 16 == 0
-            and self.kb <= self.kpad
+            and self.half % (2 * self.yb) == 0
+            and 2 * (self.width - self.half) == self.half
+            and self.columns % 2 == 0
             and self.channels % self.group == 0
             and self.tall % 16 == 0
             and self.xb % 2 == 0
@@ -210,29 +213,42 @@
 def dense_tables(plan):
     rows, columns = plan.rows, plan.columns
     eye_y = np.eye(plan.yb)
-    eye_k = np.eye(plan.kpad)[: plan.kb]
+    eye_k = np.eye(plan.kb)
     along_x = line_phase(KX, NX)
     along_y = line_phase(KY, NY)
     plane_forward, plane_inverse = plane_tables()
     tables = {}
+
+    def split(wide, axis):
+        main, left = np.split(wide, [plan.kmain], axis + 1)
+        shape = wide.shape[:axis] + (-1,) + wide.shape[axis + 4 :]
+        return np.concatenate([main.reshape(shape), left.reshape(shape)], axis)
+
     tables["plane_in"] = plane_forward.transpose(1, 2, 0).reshape(2 * KZ * KT, plan.cells)
     part = real_form(along_x.conj().T).reshape(2, rows, plan.xb, 2, columns, plan.kb)
-    wide = np.einsum("psxqgk,yw,kl->spxygqlw", part, eye_y, eye_k)
-    tables["x_in"] = wide.reshape(rows * 2 * plan.spots, columns * 2 * plan.half)
+    wide = np.einsum("psxqgk,yw->spxygkqw", part, eye_y)
+    wide = wide.reshape((rows * 2 * plan.spots,) + wide.shape[4:])
+    tables["x_in"] = split(wide, 1)
     part = real_form(along_y.conj().T).reshape(2, columns, plan.yb, 2, KY)
-    wide = np.einsum("pbyqj,kl->bplyqkj", part, eye_k)
-    wide = wide.reshape(columns * 2 * plan.half, 2, plan.modes)
+    wide = split(np.einsum("pbyqj,kl->blpyqkj", part, eye_k), 0)
+    wide = wide.reshape(columns * plan.width, 2, plan.modes)
     wide = np.pad(wide, ((0, 0), (0, 0), (0, plan.room - plan.modes)))
-    tables["y_in"] = wide.reshape(columns * 2 * plan.half, 2 * plan.room)
+    tables["y_in"] = wide.reshape(columns * plan.width, 2 * plan.room)
     part = (real_form(along_y) / NY).reshape(2, KY, 2, columns, plan.yb)
-    wide = np.einsum("pjqhy,kl->pkjhqly", part, eye_k)
-    tables["y_out"] = wide.reshape(2, plan.modes, columns * 2 * plan.half)
+    wide = split(np.einsum("pjqhy,kl->pkjhlqy", part, eye_k), 3)
+    tables["y_out"] = wide.reshape(2, plan.modes, columns * plan.width)
     part = (real_form(along_x) / NX).reshape(2, columns, plan.kb, 2, rows, plan.xb)
-    wide = np.einsum("pbkqnx,yw,kl->bplynqxw", part, eye_y, eye_k)
-    tables["x_out"] = wide.reshape(columns * 2 * plan.half, rows * 2 * plan.spots)
+    wide = split(np.einsum("pbkqnx,yw->bkpynqxw", part, eye_y), 0)
+    tables["x_out"] = wide.reshape(columns * plan.width, rows * 2 * plan.spots)
     back = plane_inverse.reshape(2, rows, plan.mb, plan.cells).transpose(1, 0, 2, 3)
     tables["plane_out"] = back.reshape(2 * KZ * KT, plan.cells)
     return {name: jnp.asarray(table.astype(jnp.bfloat16)) for name, table in tables.items()}
+
+
+def slope_twice(values):
+    scaled = values * math.sqrt(0.5)
+    bell = jnp.exp2(scaled * scaled * -math.log2(math.e))
+    return 1.0 + lax.erf(scaled) + scaled * (2.0 / math.sqrt(math.pi)) * bell
 
 
 def product(left, right, contract=((1,), (0,))):
@@ -246,6 +262,18 @@
             peer = lax.rem(lax.axis_index(axis) + hop, size)
             pl.semaphore_signal(barrier, inc=1, device_id={axis: peer}, device_id_type=MESH)
     pl.semaphore_wait(barrier, plan.rows + plan.columns - 2)
+
+
+class Tables:
+    def __init__(self, sources, places, sems):
+        self.sources, self.places, self.sems = sources, places, sems
+
+    def copy(self, index):
+        return pltpu.make_async_copy(self.sources[index], self.places[index], self.sems.at[index])
+
+    def start(self):
+        for index in range(len(self.sources)):
+            self.copy(index).start()
 
 
 class Exchange:
@@ -291,8 +319,8 @@
         pltpu.VMEM((groups, rows, tall, 2 * plan.spots), BF16),
         pltpu.SemaphoreType.DMA((groups, rows)),
         pltpu.SemaphoreType.DMA((groups, rows)),
-        pltpu.VMEM((groups, columns, tall, 2 * plan.half), BF16),
-        pltpu.VMEM((groups, columns, tall, 2 * plan.half), BF16),
+        pltpu.VMEM((groups, columns, tall + tall // 2, plan.half), BF16),
+        pltpu.VMEM((groups, columns, tall + tall // 2, plan.half), BF16),
         pltpu.SemaphoreType.DMA((groups, columns)),
         pltpu.SemaphoreType.DMA((groups, columns)),
     ]
@@ -329,18 +357,48 @@
     return jnp.concatenate([ref[group, index] for index in range(size)], 1)
 
 
+def low_lanes(rows, half):
+    return lax.broadcasted_iota(jnp.int32, (rows, half), 1) < half // 2
+
+
+def pack(plan, group, values, over_b):
+    half = plan.half
+    tall = values.shape[0]
+    low = low_lanes(tall // 2, half)
+    for pair in range(plan.columns // 2):
+        first = (plan.columns + pair) * half
+        left = values[:, first : first + half]
+        turned = pltpu.roll(left, half // 2, 1)
+        for side, (upper, lower) in enumerate(((left, turned), (turned, left))):
+            owner = 2 * pair + side
+            main = values[:, owner * half : (owner + 1) * half]
+            rest = jnp.where(low, upper[: tall // 2], lower[tall // 2 :])
+            over_b.out[group, owner] = jnp.concatenate([main, rest], 0).astype(BF16)
+    over_b.start(group)
+
+
+def unpack(plan, group, over_b):
+    over_b.arrive(group)
+    half = plan.half
+    tall = over_b.into.shape[2] * 2 // 3
+    low = low_lanes(tall // 2, half)
+    mains = [over_b.into[group, index, :tall] for index in range(plan.columns)]
+    for pair in range(plan.columns // 2):
+        first, second = [over_b.into[group, 2 * pair + side, tall:].astype(F32) for side in (0, 1)]
+        upper = jnp.where(low, first, pltpu.roll(second, half // 2, 1))
+        lower = jnp.where(low, pltpu.roll(first, half // 2, 1), second)
+        mains.append(jnp.concatenate([upper, lower], 0).astype(BF16))
+    return jnp.concatenate(mains, 1)
+
+
 def x_in(plan, group, table, over_a, over_b):
     over_a.arrive(group)
-    result = product(joined(over_a.into, group, plan.rows), table[...]).astype(BF16)
-    width = 2 * plan.half
-    for owner in range(plan.columns):
-        over_b.out[group, owner] = result[:, owner * width : (owner + 1) * width]
-    over_b.start(group)
+    result = product(joined(over_a.into, group, plan.rows), table[...])
+    pack(plan, group, result, over_b)
 
 
 def y_in(plan, group, table, over_b, sheet, real_first, imag_first):
-    over_b.arrive(group)
-    result = product(joined(over_b.into, group, plan.columns), table[...])
+    result = product(unpack(plan, group, over_b), table[...])
     mb = plan.mb
     for c in range(plan.group):
         for part in range(2):
@@ -410,21 +468,16 @@
 
 
 def y_out(plan, group, parts, table, over_b):
-    result = (product(parts[0], table[0]) + product(parts[1], table[1])).astype(BF16)
-    width = 2 * plan.half
-    tall = result.shape[0]
-    for owner in range(plan.columns):
-        cut = result[:, owner * width : (owner + 1) * width]
-        if tall < over_b.out.shape[2]:
-            over_b.out[group, owner, :tall] = cut
-        else:
-            over_b.out[group, owner] = cut
-    over_b.start(group)
+    result = product(parts[0], table[0]) + product(parts[1], table[1])
+    tall = over_b.out.shape[2] * 2 // 3
+    if result.shape[0] < tall:
+        more = jnp.zeros((tall - result.shape[0], result.shape[1]), F32)
+        result = jnp.concatenate([result, more], 0)
+    pack(plan, group, result, over_b)
 
 
 def x_out(plan, group, table, over_b, over_a):
-    over_b.arrive(group)
-    values = joined(over_b.into, group, plan.columns)
+    values = unpack(plan, group, over_b)
     width = 2 * plan.spots
     for owner in range(plan.rows):
         cut = table[:, owner * width : (owner + 1) * width]
@@ -453,16 +506,18 @@
 
 
 def forward_kernel(
-    plan, cotangent, pre, weights, t_plane, t_x, t_y, mix, skip, modes,
-    field, wide, sheet, real_first, imag_first, real_sum, imag_sum, *scratch,
+    plan, cotangent, pre, weights, h_plane, h_x, h_y, mix, skip, modes,
+    t_plane, t_x, t_y, table_sems, field, wide, sheet, real_first, imag_first, real_sum, imag_sum, *scratch,
 ):
     step = pl.program_id(0)
     over_a, over_b = exchanges(plan, scratch)
     groups, group = plan.groups, plan.group
     lanes = 512
+    tables = Tables((h_plane, h_x, h_y), (t_plane, t_x, t_y), table_sems)
 
     @pl.when(step == 0)
     def _():
+        tables.start()
         greet(plan)
         real_sum[...] = jnp.zeros_like(real_sum)
         imag_sum[...] = jnp.zeros_like(imag_sum)
@@ -474,12 +529,17 @@
             x = index % plan.xb
             for first in range(0, plan.cells, lanes):
                 cut = pl.ds(first, lanes)
-                slope = gelu_slope(pre[0, 0, c, x, :, cut].astype(F32))
-                value = cotangent[0, c, x, :, cut].astype(F32) * slope
+                slope = slope_twice(pre[0, 0, c, x, :, cut].astype(F32))
+                value = cotangent[0, c, x, :, cut].astype(F32) * 0.5 * slope
                 field[step * group + c, x, :, cut] = value.astype(BF16)
             return carry
 
-        lax.fori_loop(0, group * plan.xb, line, 0)
+        lax.fori_loop(0, group * plan.xb, line, 0, unroll=2)
+
+        @pl.when(step == 0)
+        def _():
+            tables.copy(0).wait()
+
         values = field[pl.ds(step * group, group)].reshape(group * plan.spots, plan.cells)
         plane_in(plan, step, values, t_plane, wide, over_a)
 
@@ -487,18 +547,28 @@
     def _():
         def line(index, carry):
             x = (step - groups) * (plan.xb // 2) + index
+            tile = plan.yb // 2
             for first in range(0, plan.cells, lanes):
                 cut = pl.ds(first, lanes)
-                values = field[:, x, :, cut].reshape(plan.channels * plan.yb, lanes)
-                result = product(mix[...], values).astype(BF16)
-                skip[:, index, :, cut] = result.reshape(plan.channels, plan.yb, lanes)
+                for y in (pl.ds(0, tile), pl.ds(tile, tile)):
+                    values = field[:, x, y, cut].reshape(plan.channels * tile, lanes)
+                    result = product(mix[...], values).astype(BF16)
+                    skip[:, index, y, cut] = result.reshape(plan.channels, tile, lanes)
             return carry
 
         lax.fori_loop(0, plan.xb // 2, line, 0)
 
+    @pl.when(step == 1)
+    def _():
+        tables.copy(1).wait()
+
     @pl.when(jnp.logical_and(step >= 1, step <= groups))
     def _():
         x_in(plan, step - 1, t_x, over_a, over_b)
+
+    @pl.when(step == 2)
+    def _():
+        tables.copy(2).wait()
 
     @pl.when(step >= 2)
     def _():
@@ -526,20 +596,26 @@
 
 
 def middle_kernel(
-    plan, modes, skip, pre, weights, weight, lift, t_plane, t_x, t_y, s_y, s_x, s_plane,
-    result, values, wide, field, sheet, real_first, imag_first, folded, real_sum, imag_sum,
-    *scratch,
+    plan, modes, skip, pre, weights, weight, lift, *refs,
 ):
+    (h_s_y, h_s_x, h_s_plane, h_plane, h_x, h_y, result) = refs[:7]
+    (s_y, s_x, s_plane, t_plane, t_x, t_y, table_sems) = refs[7:14]
+    (values, wide, field, sheet, real_first, imag_first, folded) = refs[14:21]
+    (real_sum, imag_sum), scratch = refs[21:23], refs[23:]
     step = pl.program_id(0)
     back_a, back_b = exchanges(plan, scratch[:8])
     over_a, over_b = exchanges(plan, scratch[8:16])
     last_a, last_b = exchanges(plan, scratch[16:])
     groups, group, tall = plan.groups, plan.group, plan.tall
     lanes = 512
+    sources = (h_s_y, h_s_x, h_s_plane, h_plane, h_x, h_y)
+    tables = Tables(sources, (s_y, s_x, s_plane, t_plane, t_x, t_y), table_sems)
 
     @pl.when(step == 0)
     def _():
+        tables.start()
         greet(plan)
+        tables.copy(0).wait()
 
         def send(index, carry):
             y_out(plan, index, (modes[index, :tall], modes[index, tall:]), s_y, back_b)
@@ -549,15 +625,24 @@
         result[...] = jnp.zeros_like(result)
         real_sum[...] = jnp.zeros_like(real_sum)
         imag_sum[...] = jnp.zeros_like(imag_sum)
+        tables.copy(1).wait()
+
+    def ahead(at, carry):
+        x_out(plan, at, s_x, back_b, back_a)
+        return carry
+
+    first = jnp.where(step == 0, 0, jnp.minimum(step + 1, groups))
+    lax.fori_loop(first, jnp.minimum(step + 2, groups), ahead, 0)
+
+    @pl.when(step == 0)
+    def _():
+        for index in range(2, 6):
+            tables.copy(index).wait()
 
     @pl.when(step < groups)
     def _():
         fold_in(plan, step, weights, lift, folded)
-        x_out(plan, step, s_x, back_b, back_a)
-
-    @pl.when(jnp.logical_and(step >= 1, step <= groups))
-    def _():
-        at = step - 1
+        at = step
         values[...] = plane_out(plan, at, group, s_plane, back_a)
 
         def line(index, carry):
@@ -568,30 +653,30 @@
             spot = pl.multiple_of(x * plan.yb, plan.yb)
             for first in range(0, plan.cells, lanes):
                 cut = pl.ds(first, lanes)
-                slope = gelu_slope(pre[0, 0, c, x, :, cut].astype(F32))
+                slope = 0.5 * slope_twice(pre[0, 0, c, x, :, cut].astype(F32))
                 incoming = values[pl.ds(row, plan.yb), cut] + skip[c, x, :, cut].astype(F32)
                 value = (incoming * slope).astype(BF16)
                 field[pl.ds(row, plan.yb), cut] = value
                 result[pl.ds(spot, plan.yb), cut] += value.astype(F32) * scale
             return carry
 
-        lax.fori_loop(0, group * plan.xb, line, 0)
+        lax.fori_loop(0, group * plan.xb, line, 0, unroll=2)
         plane_in(plan, at, field[...], t_plane, wide, over_a)
 
-    @pl.when(jnp.logical_and(step >= 2, step <= groups + 1))
-    def _():
-        x_in(plan, step - 2, t_x, over_a, over_b)
-
-    @pl.when(step >= 3)
-    def _():
-        at = step - 3
+    @pl.when(jnp.logical_and(step >= 1, step <= groups))
+    def _():
+        x_in(plan, step - 1, t_x, over_a, over_b)
+
+    @pl.when(step >= 2)
+    def _():
+        at = step - 2
         y_in(plan, at, t_y, over_b, sheet, real_first, imag_first)
         for c in range(group):
             matrix = folded[at * group + c]
             real_sum[...] += matrix * real_first[c]
             imag_sum[...] += matrix * imag_first[c]
 
-    @pl.when(step == groups + 2)
+    @pl.when(step == groups + 1)
     def _():
         rows = []
         for k in range(plan.kb):
@@ -622,6 +707,11 @@
     return pl.BlockSpec(block, lambda s: (layer, jnp.clip(s - first, 0, last), 0, 0, 0, 0))
 
 
+def table_scratch(tables, names):
+    places = [pltpu.VMEM(tables[name].shape, BF16) for name in names]
+    return places + [pltpu.SemaphoreType.DMA((len(names),))]
+
+
 def mixing_scratch(plan):
     line = (2, plan.lines)
     return [
@@ -646,9 +736,9 @@
             pl.BlockSpec((1, group) + field, lambda s: (0, at_group(s), 0, 0, 0)),
             pl.BlockSpec((1, 1, group) + field, lambda s: (layer, 0, at_group(s), 0, 0, 0)),
             weight_spec(plan, layer, 2),
-            whole(),
-            whole(),
-            whole(),
+            pl.BlockSpec(memory_space=pl.ANY),
+            pl.BlockSpec(memory_space=pl.ANY),
+            pl.BlockSpec(memory_space=pl.ANY),
             whole(),
         ],
         out_specs=[
@@ -662,7 +752,8 @@
             jax.ShapeDtypeStruct((plan.channels,) + field, BF16),
             jax.ShapeDtypeStruct((groups, 2 * plan.tall, plan.modes), BF16),
         ],
-        scratch_shapes=[
+        scratch_shapes=table_scratch(tables, ("plane_in", "x_in", "y_in"))
+        + [
             pltpu.VMEM((plan.channels,) + field, BF16),
             pltpu.VMEM((2 * KZ * KT, group * plan.spots), F32),
         ]
@@ -682,12 +773,12 @@
     sums = (plan.kb, 2, plan.lines)
 
     def at_group(step):
-        return jnp.clip(step - 1, 0, groups - 1)
-
-    names = ("plane_in", "x_in", "y_in", "y_out", "x_out", "plane_out")
+        return jnp.minimum(step, groups - 1)
+
+    names = ("y_out", "x_out", "plane_out", "plane_in", "x_in", "y_in")
     return pl.pallas_call(
         functools.partial(middle_kernel, plan),
-        grid=(groups + 3,),
+        grid=(groups + 2,),
         in_specs=[
             whole(),
             pl.BlockSpec((group,) + field, lambda s: (at_group(s), 0, 0, 0)),
@@ -696,10 +787,11 @@
             pl.BlockSpec(memory_space=pltpu.SMEM),
             pl.BlockSpec(memory_space=pltpu.SMEM),
         ]
-        + [whole()] * len(names),
+        + [pl.BlockSpec(memory_space=pl.ANY)] * len(names),
         out_specs=pl.BlockSpec((plan.spots, plan.cells), lambda s: (0, 0)),
         out_shape=jax.ShapeDtypeStruct((plan.spots, plan.cells), F32),
-        scratch_shapes=[
+        scratch_shapes=table_scratch(tables, names)
+        + [
             pltpu.VMEM((group * plan.spots, plan.cells), F32),
             pltpu.VMEM((2 * KZ * KT, group * plan.spots), F32),
             pltpu.VMEM((group * plan.spots, plan.cells), BF16),
@@ -720,7 +812,7 @@
 def per_device(plan, cotangent, pre_activations, spectral_weights, skip_weights, lift_weights):
     tables = dense_tables(plan)
     weights = spectral_weights.transpose(0, 2, 3, 4, 1, 5)
-    mix = jnp.kron(skip_weights[1].T, jnp.eye(plan.yb, dtype=BF16))
+    mix = jnp.kron(skip_weights[1].T, jnp.eye(plan.yb // 2, dtype=BF16))
     weight = jnp.sum(skip_weights[0].astype(F32) * lift_weights[None, :], 1)
     skip, modes = forward_call(plan, 1, cotangent, pre_activations, weights, tables, mix)
     result = middle_call(

time: 187 us -> 171 us (0.914)
  Pallas kernels: 180 us -> 165 us
    pallas_call x1, Pallas kernels: 115 us -> 105 us  [middle_call(): pl.pallas_call(functools.partial(middle_kernel, plan), grid=(groups + 2,)...]
    pallas_call x1, Pallas kernels: 64.9 us -> 60.3 us  [forward_call(): pl.pallas_call(functools.partial(forward_kernel, plan), grid=(groups + 2,...]
where the time goes in v3:
time: 171 us
  Pallas kernels  165 us (96%)
  local copies, waits for them, and re-layouts  4.38 us (3%)
    pallas_call x1, Pallas kernels, middle_call(): pl.pallas_call(functools.partial(middle_kernel, plan), grid=(groups + 2,)...  105 us
    pallas_call x1, Pallas kernels, forward_call(): pl.pallas_call(functools.partial(forward_kernel, plan), grid=(groups + 2,...  60.3 us

profile of v3, /device:TPU:0, one launch (start us, length us, event | category | flops | bytes accessed | tf_op | source)
XLA Modules:
  0.0 171.0 jit_solution(16273932424656994739)
XLA Ops:
  0.0 0.8 fusion.2
  0.8 1.3 fusion.weight
  2.1 0.1 copy.18
  2.2 0.1 broadcast_multiply_fusion
  2.4 1.2 mul.35.mix
  3.6 60.3 %forward.1 = (bf16[20,8,16,2048]{3,2,1,0:T(8,128)(2,1)}, bf16[5,288,144]{2,1,0:T(8,128)(2,1)}) custom-call(bf16[1,20,8,16,2048]{4,3,2,1,0:T(8,128)(2,1)} %cotangent.1, bf16[2,1,20,8,16,2048]{5,4,3,2,1,0:T(8,128)(2,1)} %pre.3, bf16[2,20,20,6,2,864]{5,4,3,2,1,0:T(2,128)(2,1)} %bitcast.11, bf16[576,2048]{1,0:T(8,128)(2,1)} %constant.14.clone.h_plane.refs_3_, ...), custom_call_target="tpu_custom_call" | custom-call | tf_op jit(solution)/shard_map/forward/pallas_call | solution.py:732
  63.9 104.8 %middle.1 = f32[128,2048]{1,0:T(8,128)} custom-call(bf16[5,288,144]{2,1,0:T(8,128)(2,1)} %get-tuple-element.7.modes, bf16[20,8,16,2048]{3,2,1,0:T(8,128)(2,1)} %get-tuple-element.8.skip, bf16[2,1,20,8,16,2048]{5,4,3,2,1,0:T(8,128)(2,1)} %pre.3, bf16[2,20,20,6,2,864]{5,4,3,2,1,0:T(2,128)(2,1)} %bitcast.12, f32[20]{0:T(128)} %fusion.weight, f32[20]{0:T(128)} %lift.1, ...), custom_call_target="tpu_custom_call" | custom-call | tf_op jit(solution)/shard_map/middle/pallas_call | solution.py:779
  168.7 2.3 %copy.23 = f32[1,8,16,2048]{3,2,1,0:T(8,128)} copy(f32[1,8,16,2048]{3,2,1,0:T(8,128)} %bitcast.13) | data formatting | bytes 2097152
  (1 shorter events, 0.0 us)

commit v4 on v3

--- a/solution.py
+++ b/solution.py
@@ -333,9 +333,8 @@
     )
 
 
-def plane_in(plan, group, values, table, wide, over_a):
+def plane_in(plan, group, wide, over_a):
     rows, mb, spots = plan.rows, plan.mb, plan.spots
-    wide[...] = product(table[...], values, ((1,), (1,)))
     for owner in range(rows):
         halves = []
         for part in range(2):
@@ -485,7 +484,7 @@
     over_a.start(group)
 
 
-def plane_out(plan, group, count, table, over_a):
+def plane_out(plan, group, count, over_a):
     over_a.arrive(group)
     mb, spots = plan.mb, plan.spots
     pieces = []
@@ -501,13 +500,12 @@
                     1,
                 )
             )
-    values = jnp.concatenate(pieces, 0).astype(BF16)
-    return product(values, table[...], ((0,), (0,)))
+    return jnp.concatenate(pieces, 0).astype(BF16)
 
 
 def forward_kernel(
-    plan, cotangent, pre, weights, h_plane, h_x, h_y, mix, skip, modes,
-    t_plane, t_x, t_y, table_sems, field, wide, sheet, real_first, imag_first, real_sum, imag_sum, *scratch,
+    plan, cotangent, pre, weights, h_plane, h_x, h_y, weight, skip, modes,
+    t_plane, t_x, t_y, table_sems, mix, field, wide, sheet, real_first, imag_first, real_sum, imag_sum, *scratch,
 ):
     step = pl.program_id(0)
     over_a, over_b = exchanges(plan, scratch)
@@ -524,24 +522,38 @@
 
     @pl.when(step < groups)
     def _():
-        def line(index, carry):
-            c = index // plan.xb
-            x = index % plan.xb
-            for first in range(0, plan.cells, lanes):
-                cut = pl.ds(first, lanes)
-                slope = slope_twice(pre[0, 0, c, x, :, cut].astype(F32))
-                value = cotangent[0, c, x, :, cut].astype(F32) * 0.5 * slope
-                field[step * group + c, x, :, cut] = value.astype(BF16)
-            return carry
-
-        lax.fori_loop(0, group * plan.xb, line, 0, unroll=2)
+        def fields(c):
+            for x in range(plan.xb):
+                for first in range(0, plan.cells, lanes):
+                    cut = pl.ds(first, lanes)
+                    slope = slope_twice(pre[0, 0, c, x, :, cut].astype(F32))
+                    value = cotangent[0, c, x, :, cut].astype(F32) * 0.5 * slope
+                    field[step * group + c, x, :, cut] = value.astype(BF16)
 
         @pl.when(step == 0)
         def _():
             tables.copy(0).wait()
 
-        values = field[pl.ds(step * group, group)].reshape(group * plan.spots, plan.cells)
-        plane_in(plan, step, values, t_plane, wide, over_a)
+        for pair in range(0, group, 2):
+            fields(pair)
+            fields(pair + 1)
+            values = field[pl.ds(step * group + pair, 2)].reshape(2 * plan.spots, plan.cells)
+            lane = pl.ds(pair * plan.spots, 2 * plan.spots)
+            wide[:, lane] = product(t_plane[...], values, ((1,), (1,)))
+        plane_in(plan, step, wide, over_a)
+
+    @pl.when(step == groups)
+    def _():
+        tile = plan.yb // 2
+        wide_rows = plan.channels * tile
+        row = lax.broadcasted_iota(jnp.int32, (wide_rows, plan.channels), 0)
+        column = lax.broadcasted_iota(jnp.int32, (wide_rows, plan.channels), 1)
+        spread = (row // tile == column).astype(F32).astype(BF16)
+        tall = product(spread, weight[1], ((1,), (1,))).astype(BF16)
+        full = product(tall, spread, ((1,), (1,)))
+        row = lax.broadcasted_iota(jnp.int32, full.shape, 0)
+        column = lax.broadcasted_iota(jnp.int32, full.shape, 1)
+        mix[...] = jnp.where(row % tile == column % tile, full, 0.0).astype(BF16)
 
     @pl.when(step >= groups)
     def _():
@@ -596,12 +608,12 @@
 
 
 def middle_kernel(
-    plan, modes, skip, pre, weights, weight, lift, *refs,
+    plan, modes, skip, pre, weights, weight, lift, lift_row, *refs,
 ):
     (h_s_y, h_s_x, h_s_plane, h_plane, h_x, h_y, result) = refs[:7]
     (s_y, s_x, s_plane, t_plane, t_x, t_y, table_sems) = refs[7:14]
-    (values, wide, field, sheet, real_first, imag_first, folded) = refs[14:21]
-    (real_sum, imag_sum), scratch = refs[21:23], refs[23:]
+    (lifted, packed, values, wide, field, sheet, real_first, imag_first) = refs[14:22]
+    (folded, real_sum, imag_sum), scratch = refs[22:25], refs[25:]
     step = pl.program_id(0)
     back_a, back_b = exchanges(plan, scratch[:8])
     over_a, over_b = exchanges(plan, scratch[8:16])
@@ -623,6 +635,8 @@
 
         lax.fori_loop(0, groups, send, 0)
         result[...] = jnp.zeros_like(result)
+        combined = jnp.sum(weight[0].astype(F32) * lift_row[...], 1, keepdims=True)
+        lifted[...] = jnp.broadcast_to(combined, lifted.shape)
         real_sum[...] = jnp.zeros_like(real_sum)
         imag_sum[...] = jnp.zeros_like(imag_sum)
         tables.copy(1).wait()
@@ -643,25 +657,40 @@
     def _():
         fold_in(plan, step, weights, lift, folded)
         at = step
-        values[...] = plane_out(plan, at, group, s_plane, back_a)
-
-        def line(index, carry):
-            c = index // plan.xb
-            x = index % plan.xb
-            scale = weight[at * group + c]
-            row = pl.multiple_of(index * plan.yb, plan.yb)
-            spot = pl.multiple_of(x * plan.yb, plan.yb)
-            for first in range(0, plan.cells, lanes):
-                cut = pl.ds(first, lanes)
-                slope = 0.5 * slope_twice(pre[0, 0, c, x, :, cut].astype(F32))
-                incoming = values[pl.ds(row, plan.yb), cut] + skip[c, x, :, cut].astype(F32)
-                value = (incoming * slope).astype(BF16)
-                field[pl.ds(row, plan.yb), cut] = value
-                result[pl.ds(spot, plan.yb), cut] += value.astype(F32) * scale
-            return carry
-
-        lax.fori_loop(0, group * plan.xb, line, 0, unroll=2)
-        plane_in(plan, at, field[...], t_plane, wide, over_a)
+        packed[...] = plane_out(plan, at, group, back_a)
+
+        def spread(part):
+            cut = pl.ds(part * lanes, lanes)
+            values[:, cut] = product(packed[...], s_plane[:, cut], ((0,), (0,)))
+
+        def fields(part):
+            cut = pl.ds(part * lanes, lanes)
+            for c in range(group):
+                scale = lifted[pl.ds(at * group + c, 1), :]
+                for x in range(plan.xb):
+                    row = pl.ds((c * plan.xb + x) * plan.yb, plan.yb)
+                    spot = pl.ds(x * plan.yb, plan.yb)
+                    slope = 0.5 * slope_twice(pre[0, 0, c, x, :, cut].astype(F32))
+                    incoming = values[row, cut] + skip[c, x, :, cut].astype(F32)
+                    value = (incoming * slope).astype(BF16)
+                    field[row, cut] = value
+                    result[spot, cut] += value.astype(F32) * scale
+
+        def gather(part):
+            cut = pl.ds(2 * part * lanes, 2 * lanes)
+            return product(t_plane[:, cut], field[:, cut], ((1,), (1,)))
+
+        spread(0)
+        spread(1)
+        fields(0)
+        spread(2)
+        fields(1)
+        wide[...] = gather(0)
+        spread(3)
+        fields(2)
+        fields(3)
+        wide[...] += gather(1)
+        plane_in(plan, at, wide, over_a)
 
     @pl.when(jnp.logical_and(step >= 1, step <= groups))
     def _():
@@ -687,7 +716,8 @@
         parts = [sheet_rows(plan, sheet, p * mb, (p + 1) * mb) for p in range(2)]
         y_out(plan, 0, parts, s_y, last_b)
         x_out(plan, 0, s_x, last_b, last_a)
-        result[...] += plane_out(plan, 0, 1, s_plane, last_a)
+        values_last = plane_out(plan, 0, 1, last_a)
+        result[...] += product(values_last, s_plane[...], ((0,), (0,)))
         for each in (back_a, back_b, over_a, over_b):
             each.finish(groups)
         for each in (last_a, last_b):
@@ -721,7 +751,7 @@
     ]
 
 
-def forward_call(plan, layer, cotangent, pre_activations, weights, tables, mix):
+def forward_call(plan, layer, cotangent, pre_activations, weights, tables, skip_weights):
     groups, group = plan.groups, plan.group
     field = (plan.xb, plan.yb, plan.cells)
     sums = (plan.channels, plan.kb, 2, plan.lines)
@@ -754,6 +784,7 @@
         ],
         scratch_shapes=table_scratch(tables, ("plane_in", "x_in", "y_in"))
         + [
+            pltpu.VMEM((plan.channels * plan.yb // 2,) * 2, BF16),
             pltpu.VMEM((plan.channels,) + field, BF16),
             pltpu.VMEM((2 * KZ * KT, group * plan.spots), F32),
         ]
@@ -764,7 +795,7 @@
             collective_id=1, has_side_effects=True, vmem_limit_bytes=VMEM_LIMIT
         ),
         name="forward",
-    )(cotangent, pre_activations, weights, tables["plane_in"], tables["x_in"], tables["y_in"], mix)
+    )(cotangent, pre_activations, weights, tables["plane_in"], tables["x_in"], tables["y_in"], skip_weights)
 
 
 def middle_call(plan, layer, modes, skip, pre_activations, weights, weight, lift, tables):
@@ -784,14 +815,17 @@
             pl.BlockSpec((group,) + field, lambda s: (at_group(s), 0, 0, 0)),
             pl.BlockSpec((1, 1, group) + field, lambda s: (layer, 0, at_group(s), 0, 0, 0)),
             weight_spec(plan, layer, 0),
+            whole(),
             pl.BlockSpec(memory_space=pltpu.SMEM),
-            pl.BlockSpec(memory_space=pltpu.SMEM),
+            whole(),
         ]
         + [pl.BlockSpec(memory_space=pl.ANY)] * len(names),
         out_specs=pl.BlockSpec((plan.spots, plan.cells), lambda s: (0, 0)),
         out_shape=jax.ShapeDtypeStruct((plan.spots, plan.cells), F32),
         scratch_shapes=table_scratch(tables, names)
         + [
+            pltpu.VMEM((plan.channels, 512), F32),
+            pltpu.VMEM((2 * KZ * KT, group * plan.spots), BF16),
             pltpu.VMEM((group * plan.spots, plan.cells), F32),
             pltpu.VMEM((2 * KZ * KT, group * plan.spots), F32),
             pltpu.VMEM((group * plan.spots, plan.cells), BF16),
@@ -806,17 +840,18 @@
             collective_id=2, has_side_effects=True, vmem_limit_bytes=VMEM_LIMIT
         ),
         name="middle",
-    )(modes, skip, pre_activations, weights, weight, lift, *[tables[name] for name in names])
+    )(
+        modes, skip, pre_activations, weights, weight, lift, lift.reshape(1, -1),
+        *[tables[name] for name in names],
+    )
 
 
 def per_device(plan, cotangent, pre_activations, spectral_weights, skip_weights, lift_weights):
     tables = dense_tables(plan)
     weights = spectral_weights.transpose(0, 2, 3, 4, 1, 5)
-    mix = jnp.kron(skip_weights[1].T, jnp.eye(plan.yb // 2, dtype=BF16))
-    weight = jnp.sum(skip_weights[0].astype(F32) * lift_weights[None, :], 1)
-    skip, modes = forward_call(plan, 1, cotangent, pre_activations, weights, tables, mix)
+    skip, modes = forward_call(plan, 1, cotangent, pre_activations, weights, tables, skip_weights)
     result = middle_call(
-        plan, 0, modes, skip, pre_activations, weights, weight, lift_weights, tables
+        plan, 0, modes, skip, pre_activations, weights, skip_weights, lift_weights, tables
     )
     return result.reshape(1, plan.xb, plan.yb, plan.cells)
 

time: 171 us -> 164 us (0.959)
  Pallas kernels: 165 us -> 160 us
    pallas_call x1, Pallas kernels: 105 us -> 102 us  [middle_call(): pl.pallas_call(functools.partial(middle_kernel, plan), grid=(groups + 2,)...]
    pallas_call x1, Pallas kernels: 60.3 us -> 58.2 us  [forward_call(): pl.pallas_call(functools.partial(forward_kernel, plan), grid=(groups + 2,...]
    unnamed x1 -> x2, local copies, waits for them, and re-layouts: 2.3 us -> 3.6 us
where the time goes in v4:
time: 164 us
  Pallas kernels  160 us (98%)
  local copies, waits for them, and re-layouts  3.6 us (2%)
    pallas_call x1, Pallas kernels, middle_call(): pl.pallas_call(functools.partial(middle_kernel, plan), grid=(groups + 2,)...  102 us
    pallas_call x1, Pallas kernels, forward_call(): pl.pallas_call(functools.partial(forward_kernel, plan), grid=(groups + 2,...  58.2 us
    unnamed x2, local copies, waits for them, and re-layouts  3.6 us

profile of v4, /device:TPU:0, one launch (start us, length us, event | category | flops | bytes accessed | tf_op | source)
XLA Modules:
  0.0 163.8 jit_solution(11701500989401516426)
XLA Ops:
  0.0 1.3 copy.12.weight
  1.3 58.2 %forward.1 = (bf16[20,8,16,2048]{3,2,1,0:T(8,128)(2,1)}, bf16[5,288,144]{2,1,0:T(8,128)(2,1)}) custom-call(bf16[1,20,8,16,2048]{4,3,2,1,0:T(8,128)(2,1)} %cotangent.1, bf16[2,1,20,8,16,2048]{5,4,3,2,1,0:T(8,128)(2,1)} %pre.3, bf16[2,20,20,6,2,864]{5,4,3,2,1,0:T(2,128)(2,1)} %bitcast.3, bf16[576,2048]{1,0:T(8,128)(2,1)} %constant.12.clone.h_plane.refs_3_, ...), custom_call_target="tpu_custom_call" | custom-call | tf_op jit(solution)/shard_map/forward/pallas_call | solution.py:762
  59.5 102.0 %middle.1 = f32[128,2048]{1,0:T(8,128)} custom-call(bf16[5,288,144]{2,1,0:T(8,128)(2,1)} %get-tuple-element.7.modes, bf16[20,8,16,2048]{3,2,1,0:T(8,128)(2,1)} %get-tuple-element.8.skip, bf16[2,1,20,8,16,2048]{5,4,3,2,1,0:T(8,128)(2,1)} %pre.3, bf16[2,20,20,6,2,864]{5,4,3,2,1,0:T(2,128)(2,1)} %bitcast.4, bf16[2,20,20]{2,1,0:T(8,128)(2,1)} %copy.12.weight, ...), custom_call_target="tpu_custom_call" | custom-call | tf_op jit(solution)/shard_map/middle/pallas_call | solution.py:810
  161.5 2.3 %copy.15 = f32[1,8,16,2048]{3,2,1,0:T(8,128)} copy(f32[1,8,16,2048]{3,2,1,0:T(8,128)} %bitcast.5) | data formatting | bytes 2097152
